TPU v7x, 32 devices: a 4x2x2 block of a 4x4x8 slice. The times are simulated.
32 devices in a mesh: dp: 4 (over y, z), ep: 8 (over x, core).
Axes of the slice: x: 4, y: 2, z: 2, core: 2. Of those that a mesh axis runs over, the one named last changes fastest.
The devices are a block of a 4x4x8 slice.
Arguments:
- grad_y: bfloat16 [4096, 1024], P(('dp', 'ep')), parts along dimension 0
- gate_vals: float32 [4096, 8], P(('dp', 'ep')), parts along dimension 0
- topk_idx: int32 [4096, 8], P(('dp', 'ep')), parts along dimension 0
- slot_ids: int32 [4096, 8], P(('dp', 'ep')), parts along dimension 0
- pair_counts: int32 [32, 32], P(('dp', 'ep')), parts along dimension 0
- y_routed: bfloat16 [4096, 8, 1024], P(('dp', 'ep')), parts along dimension 0
- x_disp: bfloat16 [128, 512, 1024], P(('dp', 'ep')), parts along dimension 0
- h_gate: bfloat16 [128, 512, 512], P(('dp', 'ep')), parts along dimension 0
- h_up: bfloat16 [128, 512, 512], P(('dp', 'ep')), parts along dimension 0
- w_gate: bfloat16 [32, 1024, 512], P('ep')
- w_up: bfloat16 [32, 1024, 512], P('ep')
- w_down: bfloat16 [32, 512, 1024], P('ep')
Outputs:
- output 1: bfloat16 [4096, 1024], P(('dp', 'ep')), parts along dimension 0
- output 2: float32 [4096, 8], P(('dp', 'ep')), parts along dimension 0
- output 3: float32 [128, 1024, 512], P(('dp', 'ep')), parts along dimension 0
- output 4: float32 [128, 1024, 512], P(('dp', 'ep')), parts along dimension 0
- output 5: float32 [128, 512, 1024], P(('dp', 'ep')), parts along dimension 0
There are 4 independent parts. A program takes and returns all parts, laid end to end along the dimension named above; an argument that names none is the same for every part.
All inputs are finite; a program needn't handle non-finite values.
Results may differ from a plain program's by a relative error of at most 0.014959.
Values are sent between devices in bfloat16 or wider.
A program may use at most 768 MiB of HBM per device.

v0:
```python
import jax
import jax.numpy as jnp
from jax import lax
from jax.sharding import PartitionSpec as P


def build_send(grad_y, gate_vals, topk_idx, slot_ids, n_exp, cap_rows):
    tok_dev, top_k = topk_idx.shape
    dest_row = jnp.where(slot_ids >= 0, topk_idx * cap_rows + slot_ids, n_exp * cap_rows).reshape(-1)
    row_source = jnp.full((n_exp * cap_rows,), tok_dev * top_k, jnp.int32).at[dest_row].set(jnp.arange(tok_dev * top_k, dtype=jnp.int32), mode="drop")
    dy_rows = jnp.take(grad_y, row_source // top_k, axis=0, mode="fill", fill_value=0)
    gate_rows = jnp.take(gate_vals.reshape(-1), row_source, mode="fill", fill_value=0)
    return (gate_rows[:, None] * dy_rows).astype(jnp.bfloat16).reshape(n_exp, cap_rows, grad_y.shape[1])


def gather_back(ret_rows, topk_idx, slot_ids, cap_rows):
    tok_dev, top_k = topk_idx.shape
    src_row = jnp.where(slot_ids >= 0, topk_idx * cap_rows + slot_ids, ret_rows.shape[0]).reshape(-1)
    picked = jnp.take(ret_rows, src_row, axis=0, mode="fill", fill_value=0).reshape(tok_dev, top_k, ret_rows.shape[1])
    return jnp.sum(picked, axis=1, dtype=jnp.float32).astype(jnp.bfloat16)


def expert_grads(grad_rows, x_rows, hg_rows, hu_rows, w_gate, w_up, w_down):
    grad_hidden = jnp.einsum("erd,efd->erf", grad_rows, w_down, preferred_element_type=jnp.float32).astype(jnp.bfloat16)
    gate_f = hg_rows.astype(jnp.float32)
    up_f = hu_rows.astype(jnp.float32)
    gate_sig = jax.nn.sigmoid(gate_f)
    gate_act = gate_f * gate_sig
    hidden_act = (gate_act * up_f).astype(jnp.bfloat16)
    grad_h = grad_hidden.astype(jnp.float32)
    grad_hgate = (grad_h * up_f * gate_sig * (1.0 + gate_f * (1.0 - gate_sig))).astype(jnp.bfloat16)
    grad_hup = (grad_h * gate_act).astype(jnp.bfloat16)
    grad_wdown = jnp.einsum("erf,erd->efd", hidden_act, grad_rows, preferred_element_type=jnp.float32)
    grad_wgate = jnp.einsum("erd,erf->edf", x_rows, grad_hgate, preferred_element_type=jnp.float32)
    grad_wup = jnp.einsum("erd,erf->edf", x_rows, grad_hup, preferred_element_type=jnp.float32)
    grad_disp = (jnp.einsum("erf,edf->erd", grad_hgate, w_gate, preferred_element_type=jnp.float32) + jnp.einsum("erf,edf->erd", grad_hup, w_up, preferred_element_type=jnp.float32)).astype(jnp.bfloat16)
    return grad_disp, grad_wgate, grad_wup, grad_wdown


def solution(mesh):
    n_dev = mesh.shape["ep"]
    rows_spec = P(("dp", "ep"), None)
    cube_spec = P(("dp", "ep"), None, None)
    weight_spec = P("ep", None, None)

    def local_step(grad_y, gate_vals, topk_idx, slot_ids, pair_counts, y_routed, x_disp, h_gate, h_up, w_gate, w_up, w_down):
        n_loc = w_gate.shape[0]
        n_exp = n_loc * n_dev
        cap_rows = x_disp.shape[1] // n_dev
        model_dim = grad_y.shape[1]
        grad_gate = jnp.einsum("td,tkd->tk", grad_y, y_routed, preferred_element_type=jnp.float32)
        send_rows = build_send(grad_y, gate_vals, topk_idx, slot_ids, n_exp, cap_rows)
        recv_rows = lax.all_to_all(send_rows.reshape(n_dev, n_loc, cap_rows, model_dim), "ep", 0, 1)
        recv_counts = lax.all_to_all(pair_counts.reshape(n_dev, n_loc), "ep", 0, 1)
        keep_row = lax.broadcasted_iota(jnp.int32, (n_loc, n_dev, cap_rows), 2) < recv_counts[:, :, None]
        grad_rows = jnp.where(keep_row[..., None], recv_rows, jnp.zeros((), jnp.bfloat16)).reshape(n_loc, n_dev * cap_rows, model_dim)
        grad_disp, grad_wgate, grad_wup, grad_wdown = expert_grads(grad_rows, x_disp, h_gate, h_up, w_gate, w_up, w_down)
        ret_rows = lax.all_to_all(grad_disp.reshape(n_loc, n_dev, cap_rows, model_dim), "ep", 1, 0)
        grad_x = gather_back(ret_rows.reshape(n_exp * cap_rows, model_dim), topk_idx, slot_ids, cap_rows)
        return grad_x, grad_gate, grad_wgate, grad_wup, grad_wdown

    return jax.shard_map(local_step, mesh=mesh, in_specs=(rows_spec, rows_spec, rows_spec, rows_spec, rows_spec, cube_spec, cube_spec, cube_spec, cube_spec, weight_spec, weight_spec, weight_spec), out_specs=(rows_spec, rows_spec, cube_spec, cube_spec, cube_spec), check_vma=False)
```

profile of v0, /device:TPU:81, one launch (start us, length us, event | category | flops | bytes accessed | tf_op | source)
XLA Modules:
  0.0 185.2 jit_solution(9397700312776309424)
XLA Ops:
  1.2 1.4 reduce.4
  3.3 6.0 %all-to-all-start = ((s32[8,4,1]{1,2,0:T(1,128)}), s32[8,4,1]{1,2,0:T(1,128)S(1)}, u32[]{:S(2)}, u32[]{:S(2)}) async-start(s32[8,4,1]{1,2,0:T(1,128)} %bitcast), calls=%async_computation | async-start | bytes 8192 | tf_op jit(solution)/shard_map/all_to_all | solution.py:54
  10.2 4.3 %scatter_custom_fusion = s32[2048]{0:T(1024)S(1)} fusion(s32[1024]{0:T(1024)S(1)} %bitcast.42, s32[1024]{0:T(1024)S(1)} %iota.18, s32[]{:T(128)} %constant.61.clone.1), kind=kCustom, calls=%fused_computation.48 | custom fusion | bytes 8196 | tf_op jit(solution)/shard_map/scatter | solution.py:10
  15.5 8.6 %gather_fusion = f32[2048]{0:T(1024)S(1)} fusion(f32[1024]{0:T(1024)S(1)} %reshape.116, s32[2048]{0:T(1024)S(1)} %get-tuple-element.27), kind=kCustom, calls=%fused_computation | custom fusion | bytes 24576 | tf_op jit(solution)/shard_map/jit(_take)/gather | solution.py:12
  24.2 9.6 %gather_fusion.1 = bf16[2048,1024]{1,0:T(8,128)(2,1)} fusion(bf16[128,1024]{1,0:T(8,128)(2,1)S(1)} %copy-done.2, s32[2048]{0:T(1024)S(1)} %get-tuple-element.28), kind=kCustom, calls=%fused_computation.1 | custom fusion | bytes 8396800 | tf_op jit(solution)/shard_map/jit(_take)/gather | solution.py:11
  33.9 4.2 %multiply_convert_fusion = bf16[8,4,1,64,1024]{4,3,1,2,0:T(8,128)(2,1)} fusion(bf16[8,4,1,64,1024]{4,3,1,2,0:T(8,128)(2,1)} %bitcast.38, f32[8,4,64]{2,1,0:T(4,128)S(1)} %mul.43, pred[8,4,64]{2,1,0:T(4,128)(4,1)S(1)} %broadcast_in_dim.61), kind=kLoop, calls=%fused_computation.5 | loop fusion | flops 8388608 | bytes 8398848 | tf_op jit(solution)/shard_map/convert_element_type | solution.py:13
  38.0 4.8 %all-to-all-start.1 = ((bf16[8,4,1,64,1024]{4,3,1,2,0:T(8,128)(2,1)}), bf16[8,4,1,64,1024]{4,3,1,2,0:T(8,128)(2,1)}, u32[]{:S(2)}, u32[]{:S(2)}) async-start(bf16[8,4,1,64,1024]{4,3,1,2,0:T(8,128)(2,1)} %multiply_convert_fusion), calls=%async_computation.1 | async-start | bytes 8388608 | tf_op jit(solution)/shard_map/all_to_all | solution.py:53
  43.1 1.4 fusion.16
  45.4 46.1 %all-to-all-done.1 = bf16[8,4,1,64,1024]{4,3,1,2,0:T(8,128)(2,1)} async-done(((bf16[8,4,1,64,1024]{4,3,1,2,0:T(8,128)(2,1)}), bf16[8,4,1,64,1024]{4,3,1,2,0:T(8,128)(2,1)}, u32[]{:S(2)}, u32[]{:S(2)}) %all-to-all-start.1) | async-done | bytes 4194336 | tf_op jit(solution)/shard_map/all_to_all | solution.py:53
  91.4 2.9 %copy.55 = bf16[8,4,1,64,1024]{4,3,0,1,2:T(8,128)(2,1)S(1)} copy(bf16[8,4,1,64,1024]{4,3,1,2,0:T(8,128)(2,1)} %all-to-all-done.1) | data formatting | bytes 8388608 | tf_op jit(solution)/shard_map/all_to_all | solution.py:53
  94.3 2.0 %copy-done.3 = bf16[8,4,1,64,1024]{4,3,0,1,2:T(8,128)(2,1)} copy-done((bf16[8,4,1,64,1024]{4,3,0,1,2:T(8,128)(2,1)}, bf16[8,4,1,64,1024]{4,3,0,1,2:T(8,128)(2,1)S(1)}, u32[]{:S(2)}) %copy-start.3) | copy-done | bytes 4194328
  96.3 3.6 %fusion.15 = bf16[4,512,512]{2,1,0:T(8,128)(2,1)} fusion(bf16[4,512,1024]{2,1,0:T(8,128)(2,1)S(1)} %copy-done.4, bf16[4,512,1024]{2,1,0:T(8,128)(2,1)S(1)} %bitcast.39, pred[4,512]{1,0:T(4,128)(4,1)S(1)} %broadcast_compare_fusion), kind=kOutput, calls=%fused_computation.30 | convolution fusion | flops 2150629376 | bytes 10487808 | tf_op jit(solution)/shard_map/erd,efd->erf/dot_general | solution.py:24
  100.5 8.2 %fusion.29 = f32[4,512,1024]{2,1,0:T(8,128)} fusion(bf16[4,1024,512]{2,1,0:T(8,128)(2,1)S(1)} %copy-done.5, bf16[4,512,512]{2,1,0:T(8,128)(2,1)S(1)} %copy-done.7, bf16[4,512,512]{2,1,0:T(8,128)(2,1)} %fusion.15, bf16[4,512,512]{2,1,0:T(8,128)(2,1)S(1)} %copy-done.8), kind=kOutput, calls=%fused_computation.57 | convolution fusion | flops 2161115136 | bytes 18874368 | tf_op jit(solution)/shard_map/erf,edf->erd/dot_general | solution.py:36
  108.7 7.2 %add_convert_fusion = bf16[4,512,1024]{2,1,0:T(8,128)(2,1)S(1)} fusion(f32[4,512,1024]{2,1,0:T(8,128)} %fusion.29, bf16[4,1024,512]{2,1,0:T(8,128)(2,1)S(1)} %copy-done.6, bf16[4,512,512]{2,1,0:T(8,128)(2,1)} %fusion.15, bf16[4,512,512]{2,1,0:T(8,128)(2,1)} %param.19), kind=kOutput, calls=%fused_computation.4 | convolution fusion | flops 2160066560 | bytes 20971520 | tf_op jit(solution)/shard_map/erf,edf->erd/dot_general | solution.py:36
  116.0 2.7 %copy.56 = bf16[1,4,8,64,1024]{4,3,1,0,2:T(8,128)(2,1)} copy(bf16[1,4,8,64,1024]{4,3,2,1,0:T(8,128)(2,1)S(1)} %bitcast.41) | data formatting | bytes 8388608 | tf_op jit(solution)/shard_map/broadcast_in_dim;reshape | solution.py:58
  118.7 5.5 %all-to-all-start.2 = ((bf16[1,4,8,64,1024]{4,3,1,0,2:T(8,128)(2,1)}), bf16[1,4,8,64,1024]{4,3,1,0,2:T(8,128)(2,1)}, u32[]{:S(2)}, u32[]{:S(2)}) async-start(bf16[1,4,8,64,1024]{4,3,1,0,2:T(8,128)(2,1)} %copy.56), calls=%async_computation.2 | async-start | bytes 8388608 | tf_op jit(solution)/shard_map/all_to_all | solution.py:58
  124.2 9.9 %convolution_bitcast_fusion.1 = f32[4,1024,512]{1,2,0:T(8,128)} fusion(bf16[4,512,1024]{2,1,0:T(8,128)(2,1)} %param.18, bf16[4,512,512]{2,1,0:T(8,128)(2,1)S(1)} %copy-done.7, bf16[4,512,512]{2,1,0:T(8,128)(2,1)} %fusion.15, bf16[4,512,512]{2,1,0:T(8,128)(2,1)} %param.19), kind=kOutput, calls=%fused_computation.25 | convolution fusion | flops 2161115136 | bytes 18874368 | tf_op jit(solution)/shard_map/erd,erf->edf/dot_general | solution.py:34
  134.1 8.7 %copy.60 = f32[4,1024,512]{2,1,0:T(8,128)} copy(f32[4,1024,512]{1,2,0:T(8,128)} %convolution_bitcast_fusion.1) | data formatting | bytes 16777216
  142.8 9.4 %convolution_bitcast_fusion = f32[4,1024,512]{1,2,0:T(8,128)} fusion(bf16[4,512,1024]{2,1,0:T(8,128)(2,1)} %param.18, bf16[4,512,512]{2,1,0:T(8,128)(2,1)} %fusion.15, bf16[4,512,512]{2,1,0:T(8,128)(2,1)} %param.19), kind=kOutput, calls=%fused_computation.24 | convolution fusion | flops 2155872256 | bytes 16777216 | tf_op jit(solution)/shard_map/erd,erf->edf/dot_general | solution.py:35
  152.2 8.7 %copy.61 = f32[4,1024,512]{2,1,0:T(8,128)} copy(f32[4,1024,512]{1,2,0:T(8,128)} %convolution_bitcast_fusion) | data formatting | bytes 16777216
  160.8 9.1 %fusion.9 = f32[4,512,1024]{2,1,0:T(8,128)} fusion(bf16[4,512,1024]{2,1,0:T(8,128)(2,1)} %bitcast.40, pred[4,512]{1,0:T(4,128)(4,1)S(1)} %broadcast_compare_fusion, bf16[4,512,512]{2,1,0:T(8,128)(2,1)S(1)} %copy-done.7, bf16[4,512,512]{2,1,0:T(8,128)(2,1)} %param.19), kind=kOutput, calls=%fused_computation.22 | convolution fusion | flops 2157969408 | bytes 16779264 | tf_op jit(solution)/shard_map/erf,erd->efd/dot_general | solution.py:33
  169.9 3.0 %all-to-all-done.2 = bf16[1,4,8,64,1024]{4,3,1,0,2:T(8,128)(2,1)} async-done(((bf16[1,4,8,64,1024]{4,3,1,0,2:T(8,128)(2,1)}), bf16[1,4,8,64,1024]{4,3,1,0,2:T(8,128)(2,1)}, u32[]{:S(2)}, u32[]{:S(2)}) %all-to-all-start.2) | async-done | bytes 4194336 | tf_op jit(solution)/shard_map/all_to_all | solution.py:58
  172.9 8.9 %gather_fusion.2 = bf16[1024,1024]{1,0:T(8,128)(2,1)} fusion(bf16[2048,1024]{1,0:T(8,128)(2,1)} %bitcast.13, s32[1024]{0:T(1024)S(1)} %broadcast_clamp_fusion.1), kind=kCustom, calls=%fused_computation.2 | custom fusion | bytes 4198400 | tf_op jit(solution)/shard_map/jit(_take)/gather | solution.py:19
  181.8 3.4 %fusion.12 = bf16[128,1024]{1,0:T(8,128)(2,1)} fusion(bf16[1024,1024]{1,0:T(8,128)(2,1)} %gather_fusion.2, pred[128,8]{1,0:T(8,128)(4,1)S(1)} %copy.49), kind=kLoop, calls=%fused_computation.27 | loop fusion | flops 1966080 | bytes 2360320 | tf_op jit(solution)/shard_map/reduce_sum | solution.py:20
  (41 shorter events, 5.0 us)
Async XLA Ops:
  0.6 42.4 %copy-start = (bf16[128,8,1024]{2,1,0:T(8,128)(2,1)S(1)}, bf16[128,8,1024]{2,1,0:T(8,128)(2,1)}, u32[]{:S(2)}) copy-start(bf16[128,8,1024]{2,1,0:T(8,128)(2,1)} %param.17) | copy-start | bytes 6291460
  3.3 34.8 %all-to-all-start = ((s32[8,4,1]{1,2,0:T(1,128)}), s32[8,4,1]{1,2,0:T(1,128)S(1)}, u32[]{:S(2)}, u32[]{:S(2)}) async-start(s32[8,4,1]{1,2,0:T(1,128)} %bitcast), calls=%async_computation | async-start | bytes 8192 | tf_op jit(solution)/shard_map/all_to_all | solution.py:54
  15.5 8.8 %copy-start.2 = (bf16[128,1024]{1,0:T(8,128)(2,1)S(1)}, bf16[128,1024]{1,0:T(8,128)(2,1)}, u32[]{:S(2)}) copy-start(bf16[128,1024]{1,0:T(8,128)(2,1)} %param.12) | copy-start | bytes 786436
  38.0 53.4 %all-to-all-start.1 = ((bf16[8,4,1,64,1024]{4,3,1,2,0:T(8,128)(2,1)}), bf16[8,4,1,64,1024]{4,3,1,2,0:T(8,128)(2,1)}, u32[]{:S(2)}, u32[]{:S(2)}) async-start(bf16[8,4,1,64,1024]{4,3,1,2,0:T(8,128)(2,1)} %multiply_convert_fusion), calls=%async_computation.1 | async-start | bytes 8388608 | tf_op jit(solution)/shard_map/all_to_all | solution.py:53
  91.4 4.8 %copy-start.4 = (bf16[4,512,1024]{2,1,0:T(8,128)(2,1)S(1)}, bf16[4,512,1024]{2,1,0:T(8,128)(2,1)}, u32[]{:S(2)}) copy-start(bf16[4,512,1024]{2,1,0:T(8,128)(2,1)} %param.23) | copy-start | bytes 12582916
  94.3 2.0 %copy-start.3 = (bf16[8,4,1,64,1024]{4,3,0,1,2:T(8,128)(2,1)}, bf16[8,4,1,64,1024]{4,3,0,1,2:T(8,128)(2,1)S(1)}, u32[]{:S(2)}) copy-start(bf16[8,4,1,64,1024]{4,3,0,1,2:T(8,128)(2,1)S(1)} %copy.55) | copy-start | bytes 12582916
  96.3 3.6 %copy-start.5 = (bf16[4,1024,512]{2,1,0:T(8,128)(2,1)S(1)}, bf16[4,1024,512]{2,1,0:T(8,128)(2,1)}, u32[]{:S(2)}) copy-start(bf16[4,1024,512]{2,1,0:T(8,128)(2,1)} %param.21) | copy-start | bytes 12582916
  96.3 3.6 %copy-start.7 = (bf16[4,512,512]{2,1,0:T(8,128)(2,1)S(1)}, bf16[4,512,512]{2,1,0:T(8,128)(2,1)}, u32[]{:S(2)}) copy-start(bf16[4,512,512]{2,1,0:T(8,128)(2,1)} %param.20) | copy-start | bytes 6291460
  96.3 4.2 %copy-start.8 = (bf16[4,512,512]{2,1,0:T(8,128)(2,1)S(1)}, bf16[4,512,512]{2,1,0:T(8,128)(2,1)}, u32[]{:S(2)}) copy-start(bf16[4,512,512]{2,1,0:T(8,128)(2,1)} %param.19) | copy-start | bytes 6291460
  100.5 8.2 %copy-start.6 = (bf16[4,1024,512]{2,1,0:T(8,128)(2,1)S(1)}, bf16[4,1024,512]{2,1,0:T(8,128)(2,1)}, u32[]{:S(2)}) copy-start(bf16[4,1024,512]{2,1,0:T(8,128)(2,1)} %param.22) | copy-start | bytes 12582916
  118.7 54.2 %all-to-all-start.2 = ((bf16[1,4,8,64,1024]{4,3,1,0,2:T(8,128)(2,1)}), bf16[1,4,8,64,1024]{4,3,1,0,2:T(8,128)(2,1)}, u32[]{:S(2)}, u32[]{:S(2)}) async-start(bf16[1,4,8,64,1024]{4,3,1,0,2:T(8,128)(2,1)} %copy.56), calls=%async_computation.2 | async-start | bytes 8388608 | tf_op jit(solution)/shard_map/all_to_all | solution.py:58
  172.9 12.3 %copy-start.1 = (bf16[128,8,1024]{2,1,0:T(8,128)(2,1)S(1)}, bf16[128,8,1024]{2,1,0:T(8,128)(2,1)}, u32[]{:S(2)}) copy-start(bf16[128,8,1024]{2,1,0:T(8,128)(2,1)} %param.17) | copy-start | bytes 6291460
where the time goes:
time: 186 us; the launch traced here: 185 us
  local copies, waits for them, and re-layouts  60.4 us (32%)
  waiting for transfers between devices  49 us (26%)
  matrix products  48.8 us (26%)
  starting transfers between devices  16.4 us (9%)
  other arithmetic  9.79 us (5%)
    all_to_all x1, waiting for transfers between devices, local_step(): lax.all_to_all(send_rows.reshape(n_dev, n_loc, cap_rows, model_dim), 'ep'...  46.1 us
    unnamed x22, local copies, waits for them, and re-layouts  21.2 us
    dot_general x1, matrix products, expert_grads(): jnp.einsum('erd,erf->edf', x_rows, grad_hgate, preferred_element_type=jnp...  9.89 us
    gather x1, local copies, waits for them, and re-layouts, build_send(): jnp.take(grad_y, row_source // top_k, axis=0, mode='fill', fill_value=0)  9.61 us
    dot_general x1, matrix products, expert_grads(): jnp.einsum('erd,erf->edf', x_rows, grad_hup, preferred_element_type=jnp.f...  9.4 us
    dot_general x1, matrix products, expert_grads(): jnp.einsum('erf,erd->efd', hidden_act, grad_rows, preferred_element_type=...  9.08 us
    gather x1, local copies, waits for them, and re-layouts, gather_back(): jnp.take(ret_rows, src_row, axis=0, mode='fill', fill_value=0)  8.9 us
    gather x1, local copies, waits for them, and re-layouts, build_send(): jnp.take(gate_vals.reshape(-1), row_source, mode='fill', fill_value=0)  8.58 us
  transfers between devices with their start and end apart: 3, of which 2 were waited for; matrix products, arithmetic and copies ran while one was open for 42% of the time, Pallas kernels for 0%

commit v1 on v0

v1 whole, which is shorter than its diff:
```python
import functools

import jax
import jax.numpy as jnp
from jax import lax
from jax.experimental import pallas as pl
from jax.experimental.pallas import tpu as pltpu
from jax.sharding import PartitionSpec as P

F32, BF16 = jnp.float32, jnp.bfloat16
COLS = 256
OPP, LEFT, RIGHT, OWN = range(4)


def dot_last(a, b):
    return lax.dot_general(a, b, (((1,), (1,)), ((), ())), preferred_element_type=F32)


def dot_first(a, b):
    return lax.dot_general(a, b, (((0,), (0,)), ((), ())), preferred_element_type=F32)


def exchange_kernel(axis, n_dev, topk_ref, slot_ref, gate_ref, count_ref, gy_hbm, y_hbm, hg_hbm, hu_hbm, wg_hbm, wu_hbm, wd_hbm,
                    d_out, dh_out, a_out, gg_out, right_out, left_out, own_out,
                    gy_all, route_send, route_all, y_buf, hg_buf, hu_buf, wgu_buf, wd_buf, f1_buf, s_buf, a_buf,
                    oh_buf, d_buf, dh_buf, r_buf, keep_buf, pair_send, pair_recv, hop_recv,
                    load_sem, store_sem, route_ssem, route_rsem, gy_ssem, gy_rsem, pair_ssem, pair_rsem, hop_ssem, hop_rsem):
    n_loc, n_rows, ffn = hg_hbm.shape
    tok, model = gy_hbm.shape
    top_k = topk_ref.shape[1]
    cap = n_rows // n_dev
    n_exp = n_loc * n_dev
    half = tok // 2
    pair_rows = 2 * cap
    n_chip = n_dev // 2

    me = lax.axis_index(axis)
    chip = lax.div(me, 2)
    core = me - 2 * chip
    chips = [lax.rem(chip + step, n_chip) for step in (2, n_chip - 1, 1, 0)]
    homes = [2 * c + core for c in chips]
    others = [2 * c + 1 - core for c in chips]
    opp, left, right = homes[OPP], homes[LEFT], homes[RIGHT]
    sib = others[OWN]
    top, bottom = pl.ds(0, half), pl.ds(half, half)

    barrier = pltpu.get_barrier_semaphore()
    for step in range(1, n_dev):
        pl.semaphore_signal(barrier, inc=1, device_id={axis: lax.rem(me + step, n_dev)}, device_id_type=pl.DeviceIdType.MESH)

    loads = {}

    def load(name, src, dst):
        loads[name] = pltpu.make_async_copy(src, dst, load_sem.at[len(loads)])
        loads[name].start()

    load("gy", gy_hbm, gy_all.at[me])
    for e in range(n_loc):
        load(("hg", e), hg_hbm.at[e], hg_buf.at[e])
        load(("hu", e), hu_hbm.at[e], hu_buf.at[e])
    load("y", y_hbm, y_buf)
    load("wd", wd_hbm, wd_buf)
    load("wg", wg_hbm, wgu_buf.at[:, :, pl.ds(0, ffn)])
    load("wu", wu_hbm, wgu_buf.at[:, :, pl.ds(ffn, ffn)])

    topk_t = topk_ref[...].astype(F32).T
    slot_t = slot_ref[...].astype(F32).T
    gate_t = gate_ref[...].T
    exp_iota = lax.broadcasted_iota(jnp.int32, (n_exp, tok), 0).astype(F32)
    diag = lax.broadcasted_iota(jnp.int32, (n_exp, n_exp), 0) == lax.broadcasted_iota(jnp.int32, (n_exp, n_exp), 1)
    count = jnp.sum(jnp.where(diag, count_ref[...].astype(F32), 0.0), axis=1, keepdims=True)
    slot_d = jnp.zeros((n_exp, tok), F32)
    gate_d = jnp.zeros((n_exp, tok), F32)
    for j in range(top_k):
        hit = topk_t[j : j + 1] == exp_iota
        slot_d += jnp.where(hit, slot_t[j : j + 1] + 1.0, 0.0)
        gate_d += jnp.where(hit, gate_t[j : j + 1], 0.0)
    slot_d -= 1.0
    slot_d = jnp.where(slot_d < count, slot_d, -1.0)
    for i in range(n_dev):
        route_send[i, 0:n_loc] = slot_d[i * n_loc : (i + 1) * n_loc]
        route_send[i, n_loc : 2 * n_loc] = gate_d[i * n_loc : (i + 1) * n_loc]
    route_all[me] = route_send[me]

    loads["gy"].wait()
    pl.semaphore_wait(barrier, n_dev - 1)

    def remote(src, dst, ssem, rsem, dev):
        return pltpu.make_async_remote_copy(src_ref=src, dst_ref=dst, send_sem=ssem, recv_sem=rsem, device_id={axis: dev}, device_id_type=pl.DeviceIdType.MESH)

    sends = []

    def gy_copy(block, part, send_slot, recv_slot, dev):
        ref = gy_all.at[block, part]
        return remote(ref, ref, gy_ssem.at[send_slot], gy_rsem.at[recv_slot], dev)

    def gy_send(block, part, recv_slot, dev):
        copy = gy_copy(block, part, recv_slot, recv_slot, dev)
        copy.start()
        sends.append(copy)

    def gy_wait(block, part, recv_slot):
        gy_copy(block, part, recv_slot, recv_slot, sib).wait_recv()

    gy_send(me, top, 0, right)
    gy_send(me, bottom, 2, left)
    gy_send(me, bottom, 1, right)
    gy_send(me, top, 3, left)
    gy_send(me, pl.ds(0, tok), 6, sib)
    for step in range(1, n_dev):
        dst = lax.rem(me + step, n_dev)
        copy = remote(route_send.at[dst], route_all.at[me], route_ssem.at[step - 1], route_rsem.at[step - 1], dst)
        copy.start()
        sends.append(copy)

    chunk = 32
    n_chunk = n_rows // chunk

    def factors(e):
        def body(i, carry):
            rows = pl.ds(pl.multiple_of(i * chunk, chunk), chunk)
            h1 = hg_buf[e, rows].astype(F32)
            h3 = hu_buf[e, rows].astype(F32)
            sig = jax.nn.sigmoid(h1)
            act = h1 * sig
            s_buf[e, rows] = act
            a_buf[e, rows] = (act * h3).astype(BF16)
            f1_buf[e, rows] = h3 * sig * (1.0 + h1 * (1.0 - sig))
            return carry

        loads[("hg", e)].wait()
        loads[("hu", e)].wait()
        lax.fori_loop(0, n_chunk, body, 0)

    factors(0)
    factors(1)

    gy_wait(left, top, 0)
    gy_send(left, top, 4, right)
    gy_send(left, top, 7, sib)
    gy_wait(right, bottom, 2)
    gy_send(right, bottom, 5, left)
    gy_send(right, bottom, 9, sib)

    factors(2)
    factors(3)
    store_a = pltpu.make_async_copy(a_buf, a_out, store_sem.at[4])
    store_a.start()

    gy_wait(left, bottom, 1)
    gy_send(left, bottom, 8, sib)
    gy_wait(right, top, 3)
    gy_send(right, top, 10, sib)

    loads["y"].wait()
    group = 32
    gg = jnp.zeros((top_k, tok), F32)
    tok_major = lax.broadcasted_iota(jnp.int32, (group, top_k, tok), 0)
    tok_lane = lax.broadcasted_iota(jnp.int32, (group, top_k, tok), 2)
    for i in range(tok // group):
        prod = dot_last(y_buf[pl.ds(i * group * top_k, group * top_k)], gy_all[me])
        gg += jnp.sum(jnp.where(tok_major + i * group == tok_lane, prod.reshape(group, top_k, tok), 0.0), axis=0)
    gg_out[...] = gg.T

    for step in range(1, n_dev):
        src = lax.rem(me + n_dev - step, n_dev)
        remote(route_send.at[src], route_all.at[src], route_ssem.at[step - 1], route_rsem.at[step - 1], src).wait_recv()

    gy_wait(opp, top, 4)
    gy_send(opp, top, 11, sib)
    gy_wait(opp, bottom, 5)
    gy_send(opp, bottom, 12, sib)

    slot_iota = lax.broadcasted_iota(jnp.int32, (cap, tok), 0).astype(F32)

    def build_rows(s):
        route = route_all[s]
        gates = []
        for e in range(n_loc):
            hit = route[e : e + 1] == slot_iota
            oh_buf[s, pl.ds(e * cap, cap)] = jnp.where(hit, 1.0, 0.0).astype(BF16)
            gates.append(jnp.sum(jnp.where(hit, route[n_loc + e : n_loc + e + 1], 0.0), axis=1, keepdims=True))
        gate = jnp.concatenate(gates, axis=0)
        pick = oh_buf[s]
        for n in range(0, model, COLS):
            rows = (jnp.dot(pick, gy_all[s, :, pl.ds(n, COLS)], preferred_element_type=F32) * gate).astype(BF16)
            for e in range(n_loc):
                d_buf[e, pl.ds(pl.multiple_of(s * cap, cap), cap), pl.ds(n, COLS)] = rows[e * cap : (e + 1) * cap]

    def rows_of(c):
        return pl.ds(pl.multiple_of(c * pair_rows, pair_rows), pair_rows)

    def experts(which, lo, hi):
        def body(e, carry):
            d_rows = jnp.concatenate([d_buf[e, rows_of(c)] for c in which], axis=0)
            for n in range(0, ffn, COLS):
                grad = dot_last(d_rows, wd_buf[e, pl.ds(n, COLS)]).astype(BF16).astype(F32)
                for i, c in enumerate(which):
                    part = grad[i * pair_rows : (i + 1) * pair_rows]
                    dh_buf[e, rows_of(c), pl.ds(n, COLS)] = (part * f1_buf[e, rows_of(c), pl.ds(n, COLS)]).astype(BF16)
                    dh_buf[e, rows_of(c), pl.ds(ffn + n, COLS)] = (part * s_buf[e, rows_of(c), pl.ds(n, COLS)]).astype(BF16)
            dh_rows = jnp.concatenate([dh_buf[e, rows_of(c)] for c in which], axis=0)
            out_rows = pl.ds(pl.multiple_of(e * cap, cap), cap)
            for n in range(0, model, COLS):
                ret = dot_last(dh_rows, wgu_buf[e, pl.ds(n, COLS)]).astype(BF16)
                for i, c in enumerate(which):
                    for k in range(2):
                        lo_row = i * pair_rows + k * cap
                        r_buf[2 * c + k, out_rows, pl.ds(n, COLS)] = ret[lo_row : lo_row + cap]
            return carry

        lax.fori_loop(lo, hi, body, 0)

    def sum_rows(s, dst):
        pick = oh_buf[s]
        for n in range(0, model, COLS):
            dst[:, pl.ds(n, COLS)] = dot_first(pick, r_buf[s, :, pl.ds(n, COLS)])

    stores = []

    def store_rows(role):
        rows = rows_of(chips[role])
        for k, (src, dst) in enumerate(((d_buf, d_out), (dh_buf, dh_out))):
            copy = pltpu.make_async_copy(src.at[:, rows], dst.at[:, rows], store_sem.at[5 + 2 * role + k])
            copy.start()
            stores.append(copy)

    pairs = {}

    def finish(role):
        store_rows(role)
        sum_rows(others[role], pair_send.at[role])
        pairs[role] = remote(pair_send.at[role], pair_recv.at[role], pair_ssem.at[role], pair_rsem.at[role], sib)
        pairs[role].start()
        sends.append(pairs[role])
        sum_rows(homes[role], keep_buf.at[role])

    loads["wd"].wait()
    gy_wait(others[OPP], top, 11)
    gy_wait(others[OPP], bottom, 12)
    build_rows(homes[OPP])
    build_rows(others[OPP])
    loads["wg"].wait()
    loads["wu"].wait()
    experts([chips[OPP]], 0, n_loc)
    finish(OPP)

    gy_wait(others[LEFT], top, 7)
    gy_wait(others[LEFT], bottom, 8)
    gy_wait(others[RIGHT], bottom, 9)
    gy_wait(others[RIGHT], top, 10)
    for role in (LEFT, RIGHT):
        build_rows(homes[role])
        build_rows(others[role])
    experts([chips[LEFT], chips[RIGHT]], 0, n_loc // 2)

    pairs[OPP].wait_recv()
    keep_buf[OPP] = keep_buf[OPP] + pair_recv[OPP]
    hop_right = remote(keep_buf.at[OPP, top], hop_recv.at[0], hop_ssem.at[0], hop_rsem.at[0], right)
    hop_right.start()
    hop_left = remote(keep_buf.at[OPP, bottom], hop_recv.at[1], hop_ssem.at[1], hop_rsem.at[1], left)
    hop_left.start()
    sends.extend([hop_right, hop_left])

    experts([chips[LEFT], chips[RIGHT]], n_loc // 2, n_loc)
    finish(LEFT)
    finish(RIGHT)

    gy_wait(others[OWN], pl.ds(0, tok), 6)
    build_rows(homes[OWN])
    build_rows(others[OWN])
    experts([chips[OWN]], 0, n_loc)
    finish(OWN)

    pairs[LEFT].wait_recv()
    pairs[RIGHT].wait_recv()
    right_out[bottom] = keep_buf[RIGHT, bottom] + pair_recv[RIGHT, bottom]
    left_out[top] = keep_buf[LEFT, top] + pair_recv[LEFT, top]
    pairs[OWN].wait_recv()
    own_out[...] = keep_buf[OWN] + pair_recv[OWN]
    hop_right.wait_recv()
    right_out[top] = keep_buf[RIGHT, top] + pair_recv[RIGHT, top] + hop_recv[0]
    hop_left.wait_recv()
    left_out[bottom] = keep_buf[LEFT, bottom] + pair_recv[LEFT, bottom] + hop_recv[1]

    for copy in sends:
        copy.wait_send()
    for copy in stores:
        copy.wait()
    store_a.wait()


def exchange(axis, n_dev, topk_idx, slot_ids, gate_vals, pair_counts, grad_y, y_rows, h_gate, h_up, w_gate, w_up, w_down):
    n_loc, n_rows, ffn = h_gate.shape
    tok, model = grad_y.shape
    top_k = topk_idx.shape[1]
    cap = n_rows // n_dev
    vmem = pl.BlockSpec(memory_space=pltpu.VMEM)
    hbm = pl.BlockSpec(memory_space=pl.ANY)
    dma = pltpu.SemaphoreType.DMA
    part = jax.ShapeDtypeStruct((tok, model), F32)
    return pl.pallas_call(
        functools.partial(exchange_kernel, axis, n_dev),
        name="exchange",
        out_shape=(
            jax.ShapeDtypeStruct((n_loc, n_rows, model), BF16),
            jax.ShapeDtypeStruct((n_loc, n_rows, 2 * ffn), BF16),
            jax.ShapeDtypeStruct((n_loc, n_rows, ffn), BF16),
            jax.ShapeDtypeStruct((tok, top_k), F32),
            part, part, part,
        ),
        in_specs=[vmem] * 4 + [hbm] * 7,
        out_specs=(hbm, hbm, hbm, vmem, vmem, vmem, vmem),
        scratch_shapes=[
            pltpu.VMEM((n_dev, tok, model), BF16),
            pltpu.VMEM((n_dev, 2 * n_loc, tok), F32),
            pltpu.VMEM((n_dev, 2 * n_loc, tok), F32),
            pltpu.VMEM(y_rows.shape, BF16),
            pltpu.VMEM(h_gate.shape, BF16),
            pltpu.VMEM(h_up.shape, BF16),
            pltpu.VMEM((n_loc, model, 2 * ffn), BF16),
            pltpu.VMEM(w_down.shape, BF16),
            pltpu.VMEM(h_gate.shape, F32),
            pltpu.VMEM(h_gate.shape, F32),
            pltpu.VMEM(h_gate.shape, BF16),
            pltpu.VMEM((n_dev, n_loc * cap, tok), BF16),
            pltpu.VMEM((n_loc, n_rows, model), BF16),
            pltpu.VMEM((n_loc, n_rows, 2 * ffn), BF16),
            pltpu.VMEM((n_dev, n_loc * cap, model), BF16),
            pltpu.VMEM((4, tok, model), F32),
            pltpu.VMEM((4, tok, model), F32),
            pltpu.VMEM((4, tok, model), F32),
            pltpu.VMEM((2, tok // 2, model), F32),
            dma((5 + 2 * n_loc,)), dma((13,)), dma((n_dev - 1,)), dma((n_dev - 1,)), dma((13,)), dma((13,)),
            dma((4,)), dma((4,)), dma((2,)), dma((2,)),
        ],
        compiler_params=pltpu.CompilerParams(collective_id=0, has_side_effects=True, vmem_limit_bytes=60 * 1024 * 1024),
    )(topk_idx, slot_ids, gate_vals, pair_counts, grad_y, y_rows, h_gate, h_up, w_gate, w_up, w_down)


def weight_kernel(ffn, x_ref, dh_ref, a_ref, d_ref, gg_ref, wg_out, wu_out, wd_out, gg_out):
    @pl.when((pl.program_id(0) == 0) & (pl.program_id(1) == 0))
    def _():
        gg_out[...] = gg_ref[...]

    x = x_ref[0]
    for n in range(0, ffn, COLS):
        wg_out[0, :, pl.ds(n, COLS)] = dot_first(x, dh_ref[0, :, pl.ds(n, COLS)])
        wu_out[0, :, pl.ds(n, COLS)] = dot_first(x, dh_ref[0, :, pl.ds(ffn + n, COLS)])
    a = a_ref[0]
    for n in range(0, d_ref.shape[2], COLS):
        wd_out[0, :, pl.ds(n, COLS)] = dot_first(a, d_ref[0, :, pl.ds(n, COLS)])


def weight_grads(x_disp, dh_rows, a_rows, d_rows, gg):
    n_loc, n_rows, model = x_disp.shape
    ffn = a_rows.shape[2]
    split = 2
    m_blk, f_blk = model // split, ffn // split
    flops = 2 * n_loc * n_rows * model * 3 * ffn
    moved = 2 * (x_disp.size + dh_rows.size + a_rows.size + d_rows.size) + 12 * n_loc * model * ffn
    return pl.pallas_call(
        functools.partial(weight_kernel, ffn),
        name="weight_grads",
        grid=(n_loc, split),
        in_specs=[
            pl.BlockSpec((1, n_rows, m_blk), lambda e, h: (e, 0, h)),
            pl.BlockSpec((1, n_rows, 2 * ffn), lambda e, h: (e, 0, 0)),
            pl.BlockSpec((1, n_rows, f_blk), lambda e, h: (e, 0, h)),
            pl.BlockSpec((1, n_rows, model), lambda e, h: (e, 0, 0)),
            pl.BlockSpec(gg.shape, lambda e, h: (0, 0)),
        ],
        out_specs=(
            pl.BlockSpec((1, m_blk, ffn), lambda e, h: (e, h, 0)),
            pl.BlockSpec((1, m_blk, ffn), lambda e, h: (e, h, 0)),
            pl.BlockSpec((1, f_blk, model), lambda e, h: (e, h, 0)),
            pl.BlockSpec(gg.shape, lambda e, h: (0, 0)),
        ),
        out_shape=(
            jax.ShapeDtypeStruct((n_loc, model, ffn), F32),
            jax.ShapeDtypeStruct((n_loc, model, ffn), F32),
            jax.ShapeDtypeStruct((n_loc, ffn, model), F32),
            jax.ShapeDtypeStruct(gg.shape, F32),
        ),
        cost_estimate=pl.CostEstimate(flops=flops, bytes_accessed=moved, transcendentals=0),
        compiler_params=pltpu.CompilerParams(vmem_limit_bytes=40 * 1024 * 1024),
    )(x_disp, dh_rows, a_rows, d_rows, gg)


def final_kernel(own_ref, left_ref, right_ref, gx_out):
    gx_out[...] = (own_ref[...] + left_ref[...] + right_ref[...]).astype(BF16)


def final_sum(own, from_left, from_right):
    vmem = pl.BlockSpec(memory_space=pltpu.VMEM)
    return pl.pallas_call(
        final_kernel,
        name="final_sum",
        out_shape=jax.ShapeDtypeStruct(own.shape, BF16),
        in_specs=[vmem] * 3,
        out_specs=vmem,
    )(own, from_left, from_right)


def solution(mesh):
    axis = "ep"
    n_dev = mesh.shape[axis]
    rows_spec = P(("dp", "ep"), None)
    cube_spec = P(("dp", "ep"), None, None)
    weight_spec = P("ep", None, None)
    to_right = [(i, (i + 2) % n_dev) for i in range(n_dev)]
    to_left = [(i, (i - 2) % n_dev) for i in range(n_dev)]

    def local_step(grad_y, gate_vals, topk_idx, slot_ids, pair_counts, y_routed, x_disp, h_gate, h_up, w_gate, w_up, w_down):
        y_rows = y_routed.reshape(-1, y_routed.shape[2])
        d_rows, dh_rows, a_rows, gg, for_right, for_left, own = exchange(
            axis, n_dev, topk_idx, slot_ids, gate_vals, pair_counts, grad_y, y_rows, h_gate, h_up, w_gate, w_up, w_down)
        from_left = lax.ppermute(for_right, axis, to_right)
        from_right = lax.ppermute(for_left, axis, to_left)
        grad_wgate, grad_wup, grad_wdown, grad_gate = weight_grads(x_disp, dh_rows, a_rows, d_rows, gg)
        grad_x = final_sum(own, from_left, from_right)
        return grad_x, grad_gate, grad_wgate, grad_wup, grad_wdown

    return jax.shard_map(local_step, mesh=mesh, in_specs=(rows_spec, rows_spec, rows_spec, rows_spec, rows_spec, cube_spec, cube_spec, cube_spec, cube_spec, weight_spec, weight_spec, weight_spec), out_specs=(rows_spec, rows_spec, cube_spec, cube_spec, cube_spec), check_vma=False)
```

time: 186 us -> 71.7 us (0.39)
  Pallas kernels: 0 us -> 55 us
  waiting for transfers between devices: 49 us -> 0.01 us
  matrix products: 48.8 us -> 0 us
  local copies, waits for them, and re-layouts: 60.4 us -> 12.7 us
  starting transfers between devices: 16.4 us -> 2.76 us
  other arithmetic: 9.79 us -> 0 us
    pallas_call x0 -> x3, Pallas kernels: none -> 55 us  [the longest x1 38.8 us: exchange(): pl.pallas_call(functools.partial(exchange_kernel, axis, n_dev), name='exc...]
    all_to_all x3 -> x0, waiting for transfers between devices: 49 us -> none  [the longest x1 46.1 us: local_step(): lax.all_to_all(send_rows.reshape(n_dev, n_loc, cap_rows, model_dim), 'ep'...]
    dot_general x7 -> x0, matrix products: 48.8 us -> none  [the longest x1 9.89 us: expert_grads(): jnp.einsum('erd,erf->edf', x_rows, grad_hgate, preferred_element_type=jnp...]
    gather x3 -> x0, local copies, waits for them, and re-layouts: 27.1 us -> none  [the longest x1 9.61 us: build_send(): jnp.take(grad_y, row_source // top_k, axis=0, mode='fill', fill_value=0)]
    all_to_all x3 -> x0, starting transfers between devices: 16.4 us -> none  [the longest x1 6.02 us: local_step(): recv_counts = lax.all_to_all(pair_counts.reshape(n_dev, n_loc), 'ep', 0, 1)]
    unnamed x22 -> x16, local copies, waits for them, and re-layouts: 21.2 us -> 12.7 us
    scatter x1 -> x0, local copies, waits for them, and re-layouts: 4.32 us -> none  [build_send(): jnp.full((n_exp * cap_rows,), tok_dev * top_k, jnp.int32).at[dest_row]]
    convert_element_type x1 -> x0, other arithmetic: 4.18 us -> none  [build_send(): (gate_rows[:, None] * dy_rows).astype(jnp.bfloat16)]
  transfers between devices with their start and end apart: 3 -> 2, of which waited for: 2 -> 0; matrix products, arithmetic and copies ran while one was open for 42% -> 1% of each run, Pallas kernels for 0% -> 20%
where the time goes in v1:
time: 71.7 us; the launch traced here: 71.1 us
  Pallas kernels  55 us (77%)
  local copies, waits for them, and re-layouts  12.7 us (18%)
  starting transfers between devices  2.76 us (4%)
    pallas_call x1, Pallas kernels, exchange(): pl.pallas_call(functools.partial(exchange_kernel, axis, n_dev), name='exc...  38.8 us
    pallas_call x1, Pallas kernels, weight_grads(): pl.pallas_call(functools.partial(weight_kernel, ffn), name='weight_grads'...  14.1 us
    unnamed x16, local copies, waits for them, and re-layouts  12.7 us
    pallas_call x1, Pallas kernels, final_sum(): pl.pallas_call(final_kernel, name='final_sum', out_shape=jax.ShapeDtypeSt...  2.13 us
    ppermute x1, starting transfers between devices, local_step(): from_right = lax.ppermute(for_left, axis, to_left)  1.91 us
  transfers between devices with their start and end apart: 2, of which 0 were waited for; matrix products, arithmetic and copies ran while one was open for 1% of the time, Pallas kernels for 20%

profile of v1, /device:TPU:81, one launch (start us, length us, event | category | flops | bytes accessed | tf_op | source)
XLA Modules:
  0.0 71.1 jit_solution(2685261921447837828)
XLA Ops:
  0.6 1.4 %copy.19.gate_ref = f32[128,8]{1,0:T(8,128)} copy(f32[128,8]{0,1:T(8,128)} %param.13) | data formatting | bytes 8192 | tf_op args[1]
  2.0 1.4 %copy.17.topk_ref = s32[128,8]{1,0:T(8,128)} copy(s32[128,8]{0,1:T(8,128)} %param.14) | data formatting | bytes 8192 | tf_op args[2]
  3.5 1.4 %copy.18.slot_ref = s32[128,8]{1,0:T(8,128)} copy(s32[128,8]{0,1:T(8,128)} %param.15) | data formatting | bytes 8192 | tf_op args[3]
  4.9 38.8 %exchange.1 = (bf16[4,512,1024]{2,1,0:T(8,128)(2,1)}, bf16[4,512,1024]{2,1,0:T(8,128)(2,1)}, bf16[4,512,512]{2,1,0:T(8,128)(2,1)}, f32[128,8]{1,0:T(8,128)}, f32...) custom-call(s32[128,8]{1,0:T(8,128)} %copy.17.topk_ref, s32[128,8]{1,0:T(8,128)} %copy.18.slot_ref, ...), custom_call_target="tpu_custom_call" | custom-call | tf_op jit(solution)/shard_map/exchange/pallas_call | solution.py:302
  43.7 0.9 %collective-permute-start = (f32[128,1024]{1,0:T(8,128)}, f32[128,1024]{1,0:T(8,128)S(1)}, u32[]{:S(2)}, u32[]{:S(2)}) collective-permute-start(f32[128,1024]{1,0:T(8,128)} %get-tuple-element.17), channel_id=1, source_target_pairs={{0,2},{1,3},{2,4},{3,5},{4,6},{5,7},{6,0},{7,1},{8,10},{9,11},{10,... | collective-permute-start | bytes 1572872 | tf_op jit(solution)/shard_map/ppermute | solution.py:418
  44.5 1.9 %collective-permute-start.1 = (f32[128,1024]{1,0:T(8,128)}, f32[128,1024]{1,0:T(8,128)S(1)}, u32[]{:S(2)}, u32[]{:S(2)}) collective-permute-start(f32[128,1024]{1,0:T(8,128)} %get-tuple-element.18), channel_id=1, source_target_pairs={{0,6},{1,7},{2,0},{3,1},{4,2},{5,3},{6,4},{7,5},{8,14},{9,15},{10,... | collective-permute-start | bytes 1572872 | tf_op jit(solution)/shard_map/ppermute | solution.py:419
  46.4 0.0 copy-start
  46.4 2.2 %copy-done = bf16[4,512,1024]{2,1,0:T(8,128)(2,1)S(1)} copy-done((bf16[4,512,1024]{2,1,0:T(8,128)(2,1)S(1)}, bf16[4,512,1024]{2,1,0:T(8,128)(2,1)}, u32[]{:S(2)}) %copy-start) | copy-done | bytes 4194328
  48.6 0.0 copy-start.1
  48.6 2.2 %copy-done.1 = bf16[4,512,1024]{2,1,0:T(8,128)(2,1)S(1)} copy-done((bf16[4,512,1024]{2,1,0:T(8,128)(2,1)S(1)}, bf16[4,512,1024]{2,1,0:T(8,128)(2,1)}, u32[]{:S(2)}) %copy-start.1) | copy-done | bytes 4194328
  50.8 0.0 copy-start.2
  50.8 1.6 %copy-done.2 = bf16[4,512,512]{2,1,0:T(8,128)(2,1)S(1)} copy-done((bf16[4,512,512]{2,1,0:T(8,128)(2,1)S(1)}, bf16[4,512,512]{2,1,0:T(8,128)(2,1)}, u32[]{:S(2)}) %copy-start.2) | copy-done | bytes 2097176
  52.4 0.0 copy-start.3
  52.4 0.8 %copy-done.3 = f32[128,8]{1,0:T(8,128)S(1)} copy-done((f32[128,8]{1,0:T(8,128)S(1)}, f32[128,8]{1,0:T(8,128)}, u32[]{:S(2)}) %copy-start.3) | copy-done | bytes 4120
  53.2 14.1 %weight_grads.1 = (f32[4,1024,512]{2,1,0:T(8,128)}, f32[4,1024,512]{2,1,0:T(8,128)}, f32[4,512,1024]{2,1,0:T(8,128)}, f32[128,8]{1,0:T(8,128)S(1)}) custom-call(bf16[4,512,1024]{2,1,0:T(8,128)(2,1)S(1)} %copy-done, bf16[4,512,1024]{2,1,0:T(8,128)(2,1)S(1)} %copy-done.1, bf16[4,512,512]{2,1,0:T(8,128)(2,1)S(1)} %copy-done.2, ...), custom_call_target="tpu_custom_call" | custom-call | flops 6442450944 | bytes 39845888 | tf_op jit(solution)/shard_map/weight_grads/pallas_call | solution.py:362
  67.3 0.7 copy.20
  68.0 0.0 collective-permute-done.left_ref
  68.0 0.0 copy-start.4
  68.0 0.0 collective-permute-done.1.right_ref
  68.0 0.0 copy-start.5
  68.0 0.8 %copy-done.4 = f32[128,1024]{1,0:T(8,128)} copy-done((f32[128,1024]{1,0:T(8,128)}, f32[128,1024]{1,0:T(8,128)S(1)}, u32[]{:S(2)}) %copy-start.4) | copy-done | bytes 524312
  68.8 0.2 copy-done.5
  69.0 2.1 %final_sum.1 = bf16[128,1024]{1,0:T(8,128)(2,1)} custom-call(f32[128,1024]{1,0:T(8,128)} %get-tuple-element.16.own_ref, f32[128,1024]{1,0:T(8,128)} %copy-done.4, f32[128,1024]{1,0:T(8,128)} %copy-done.5), custom_call_target="tpu_custom_call" | custom-call | tf_op jit(solution)/shard_map/final_sum/pallas_call | solution.py:396
Async XLA Ops:
  43.7 24.3 %collective-permute-start = (f32[128,1024]{1,0:T(8,128)}, f32[128,1024]{1,0:T(8,128)S(1)}, u32[]{:S(2)}, u32[]{:S(2)}) collective-permute-start(f32[128,1024]{1,0:T(8,128)} %get-tuple-element.17), channel_id=1, source_target_pairs={{0,2},{1,3},{2,4},{3,5},{4,6},{5,7},{6,0},{7,1},{8,10},{9,11},{10,... | collective-permute-start | bytes 1572872 | tf_op jit(solution)/shard_map/ppermute | solution.py:418
  44.5 23.5 %collective-permute-start.1 = (f32[128,1024]{1,0:T(8,128)}, f32[128,1024]{1,0:T(8,128)S(1)}, u32[]{:S(2)}, u32[]{:S(2)}) collective-permute-start(f32[128,1024]{1,0:T(8,128)} %get-tuple-element.18), channel_id=1, source_target_pairs={{0,6},{1,7},{2,0},{3,1},{4,2},{5,3},{6,4},{7,5},{8,14},{9,15},{10,... | collective-permute-start | bytes 1572872 | tf_op jit(solution)/shard_map/ppermute | solution.py:419
  46.4 2.2 %copy-start = (bf16[4,512,1024]{2,1,0:T(8,128)(2,1)S(1)}, bf16[4,512,1024]{2,1,0:T(8,128)(2,1)}, u32[]{:S(2)}) copy-start(bf16[4,512,1024]{2,1,0:T(8,128)(2,1)} %x_ref.1) | copy-start | bytes 12582916
  48.6 2.2 %copy-start.1 = (bf16[4,512,1024]{2,1,0:T(8,128)(2,1)S(1)}, bf16[4,512,1024]{2,1,0:T(8,128)(2,1)}, u32[]{:S(2)}) copy-start(bf16[4,512,1024]{2,1,0:T(8,128)(2,1)} %get-tuple-element.19.dh_ref) | copy-start | bytes 12582916
  50.8 1.6 %copy-start.2 = (bf16[4,512,512]{2,1,0:T(8,128)(2,1)S(1)}, bf16[4,512,512]{2,1,0:T(8,128)(2,1)}, u32[]{:S(2)}) copy-start(bf16[4,512,512]{2,1,0:T(8,128)(2,1)} %get-tuple-element.20.a_ref) | copy-start | bytes 6291460
  52.4 0.8 %copy-start.3 = (f32[128,8]{1,0:T(8,128)S(1)}, f32[128,8]{1,0:T(8,128)}, u32[]{:S(2)}) copy-start(f32[128,8]{1,0:T(8,128)} %get-tuple-element.22.gg_ref) | copy-start | bytes 12292
  68.0 0.8 %copy-start.4 = (f32[128,1024]{1,0:T(8,128)}, f32[128,1024]{1,0:T(8,128)S(1)}, u32[]{:S(2)}) copy-start(f32[128,1024]{1,0:T(8,128)S(1)} %collective-permute-done.left_ref) | copy-start | bytes 1572868
  68.0 1.0 %copy-start.5 = (f32[128,1024]{1,0:T(8,128)}, f32[128,1024]{1,0:T(8,128)S(1)}, u32[]{:S(2)}) copy-start(f32[128,1024]{1,0:T(8,128)S(1)} %collective-permute-done.1.right_ref) | copy-start | bytes 1572868

commit v2 on v1

--- a/solution.py
+++ b/solution.py
@@ -27,7 +27,7 @@
                     load_sem, store_sem, route_ssem, route_rsem, gy_ssem, gy_rsem, pair_ssem, pair_rsem, hop_ssem, hop_rsem):
     n_loc, n_rows, ffn = hg_hbm.shape
     tok, model = gy_hbm.shape
-    top_k = topk_ref.shape[1]
+    top_k = topk_ref.shape[0]
     cap = n_rows // n_dev
     n_exp = n_loc * n_dev
     half = tok // 2
@@ -63,9 +63,9 @@
     load("wg", wg_hbm, wgu_buf.at[:, :, pl.ds(0, ffn)])
     load("wu", wu_hbm, wgu_buf.at[:, :, pl.ds(ffn, ffn)])
 
-    topk_t = topk_ref[...].astype(F32).T
-    slot_t = slot_ref[...].astype(F32).T
-    gate_t = gate_ref[...].T
+    topk_t = topk_ref[...].astype(F32)
+    slot_t = slot_ref[...].astype(F32)
+    gate_t = gate_ref[...]
     exp_iota = lax.broadcasted_iota(jnp.int32, (n_exp, tok), 0).astype(F32)
     diag = lax.broadcasted_iota(jnp.int32, (n_exp, n_exp), 0) == lax.broadcasted_iota(jnp.int32, (n_exp, n_exp), 1)
     count = jnp.sum(jnp.where(diag, count_ref[...].astype(F32), 0.0), axis=1, keepdims=True)
@@ -160,7 +160,7 @@
     for i in range(tok // group):
         prod = dot_last(y_buf[pl.ds(i * group * top_k, group * top_k)], gy_all[me])
         gg += jnp.sum(jnp.where(tok_major + i * group == tok_lane, prod.reshape(group, top_k, tok), 0.0), axis=0)
-    gg_out[...] = gg.T
+    gg_out[...] = gg
 
     for step in range(1, n_dev):
         src = lax.rem(me + n_dev - step, n_dev)
@@ -293,7 +293,7 @@
 def exchange(axis, n_dev, topk_idx, slot_ids, gate_vals, pair_counts, grad_y, y_rows, h_gate, h_up, w_gate, w_up, w_down):
     n_loc, n_rows, ffn = h_gate.shape
     tok, model = grad_y.shape
-    top_k = topk_idx.shape[1]
+    top_k = topk_idx.shape[0]
     cap = n_rows // n_dev
     vmem = pl.BlockSpec(memory_space=pltpu.VMEM)
     hbm = pl.BlockSpec(memory_space=pl.ANY)
@@ -306,7 +306,7 @@
             jax.ShapeDtypeStruct((n_loc, n_rows, model), BF16),
             jax.ShapeDtypeStruct((n_loc, n_rows, 2 * ffn), BF16),
             jax.ShapeDtypeStruct((n_loc, n_rows, ffn), BF16),
-            jax.ShapeDtypeStruct((tok, top_k), F32),
+            jax.ShapeDtypeStruct((top_k, tok), F32),
             part, part, part,
         ),
         in_specs=[vmem] * 4 + [hbm] * 7,
@@ -383,7 +383,7 @@
             jax.ShapeDtypeStruct(gg.shape, F32),
         ),
         cost_estimate=pl.CostEstimate(flops=flops, bytes_accessed=moved, transcendentals=0),
-        compiler_params=pltpu.CompilerParams(vmem_limit_bytes=40 * 1024 * 1024),
+        compiler_params=pltpu.CompilerParams(vmem_limit_bytes=60 * 1024 * 1024),
     )(x_disp, dh_rows, a_rows, d_rows, gg)
 
 
@@ -399,6 +399,7 @@
         out_shape=jax.ShapeDtypeStruct(own.shape, BF16),
         in_specs=[vmem] * 3,
         out_specs=vmem,
+        compiler_params=pltpu.CompilerParams(vmem_limit_bytes=8 * 1024 * 1024),
     )(own, from_left, from_right)
 
 
@@ -414,11 +415,11 @@
     def local_step(grad_y, gate_vals, topk_idx, slot_ids, pair_counts, y_routed, x_disp, h_gate, h_up, w_gate, w_up, w_down):
         y_rows = y_routed.reshape(-1, y_routed.shape[2])
         d_rows, dh_rows, a_rows, gg, for_right, for_left, own = exchange(
-            axis, n_dev, topk_idx, slot_ids, gate_vals, pair_counts, grad_y, y_rows, h_gate, h_up, w_gate, w_up, w_down)
+            axis, n_dev, topk_idx.T, slot_ids.T, gate_vals.T, pair_counts, grad_y, y_rows, h_gate, h_up, w_gate, w_up, w_down)
         from_left = lax.ppermute(for_right, axis, to_right)
         from_right = lax.ppermute(for_left, axis, to_left)
         grad_wgate, grad_wup, grad_wdown, grad_gate = weight_grads(x_disp, dh_rows, a_rows, d_rows, gg)
         grad_x = final_sum(own, from_left, from_right)
-        return grad_x, grad_gate, grad_wgate, grad_wup, grad_wdown
+        return grad_x, grad_gate.T, grad_wgate, grad_wup, grad_wdown
 
     return jax.shard_map(local_step, mesh=mesh, in_specs=(rows_spec, rows_spec, rows_spec, rows_spec, rows_spec, cube_spec, cube_spec, cube_spec, cube_spec, weight_spec, weight_spec, weight_spec), out_specs=(rows_spec, rows_spec, cube_spec, cube_spec, cube_spec), check_vma=False)

time: 71.7 us -> 62.5 us (0.87)
  local copies, waits for them, and re-layouts: 12.7 us -> 0.01 us
  Pallas kernels: 55 us -> 58.8 us
    unnamed x16 -> x2, local copies, waits for them, and re-layouts: 12.7 us -> 0.01 us
    pallas_call x1, Pallas kernels: 14.1 us -> 19.4 us  [weight_grads(): pl.pallas_call(functools.partial(weight_kernel, ffn), name='weight_grads'...]
    pallas_call x1, Pallas kernels: 2.13 us -> 0.77 us  [final_sum(): pl.pallas_call(final_kernel, name='final_sum', out_shape=jax.ShapeDtypeSt...]
  transfers between devices with their start and end apart: 2 -> 2, of which waited for: 0 -> 0; matrix products, arithmetic and copies ran while one was open for 1% -> 0% of each run, Pallas kernels for 20% -> 31%
where the time goes in v2:
time: 62.5 us; the launch traced here: 62.3 us
  Pallas kernels  58.8 us (94%)
  starting transfers between devices  2.76 us (4%)
  between operations  0.66 us (1%)
    pallas_call x1, Pallas kernels, exchange(): pl.pallas_call(functools.partial(exchange_kernel, axis, n_dev), name='exc...  38.6 us
    pallas_call x1, Pallas kernels, weight_grads(): pl.pallas_call(functools.partial(weight_kernel, ffn), name='weight_grads'...  19.4 us
    ppermute x1, starting transfers between devices, local_step(): from_right = lax.ppermute(for_left, axis, to_left)  1.93 us
  transfers between devices with their start and end apart: 2, of which 0 were waited for; matrix products, arithmetic and copies ran while one was open for 0% of the time, Pallas kernels for 31%

profile of v2, /device:TPU:81, one launch (start us, length us, event | category | flops | bytes accessed | tf_op | source)
XLA Modules:
  0.0 62.3 jit_solution(9332229171208273992)
XLA Ops:
  0.6 38.6 %exchange.1 = (bf16[4,512,1024]{2,1,0:T(8,128)(2,1)}, bf16[4,512,1024]{2,1,0:T(8,128)(2,1)}, bf16[4,512,512]{2,1,0:T(8,128)(2,1)}, f32[8,128]{1,0:T(8,128)}, f32...) custom-call(s32[8,128]{1,0:T(8,128)} %bitcast.6, s32[8,128]{1,0:T(8,128)} %bitcast.7, ...), custom_call_target="tpu_custom_call" | custom-call | tf_op jit(solution)/shard_map/exchange/pallas_call | solution.py:302
  39.2 0.8 %collective-permute-start = (f32[128,1024]{1,0:T(8,128)}, f32[128,1024]{1,0:T(8,128)S(1)}, u32[]{:S(2)}, u32[]{:S(2)}) collective-permute-start(f32[128,1024]{1,0:T(8,128)} %get-tuple-element.17), channel_id=1, source_target_pairs={{0,2},{1,3},{2,4},{3,5},{4,6},{5,7},{6,0},{7,1},{8,10},{9,11},{10,... | collective-permute-start | bytes 1572872 | tf_op jit(solution)/shard_map/ppermute | solution.py:419
  40.1 1.9 %collective-permute-start.1 = (f32[128,1024]{1,0:T(8,128)}, f32[128,1024]{1,0:T(8,128)S(1)}, u32[]{:S(2)}, u32[]{:S(2)}) collective-permute-start(f32[128,1024]{1,0:T(8,128)} %get-tuple-element.18), channel_id=1, source_target_pairs={{0,6},{1,7},{2,0},{3,1},{4,2},{5,3},{6,4},{7,5},{8,14},{9,15},{10,... | collective-permute-start | bytes 1572872 | tf_op jit(solution)/shard_map/ppermute | solution.py:420
  42.0 0.0 copy-start
  42.0 19.4 %weight_grads.1 = (f32[4,1024,512]{2,1,0:T(8,128)}, f32[4,1024,512]{2,1,0:T(8,128)}, f32[4,512,1024]{2,1,0:T(8,128)}, f32[8,128]{1,0:T(8,128)}) custom-call(bf16[4,512,1024]{2,1,0:T(8,128)(2,1)} %x_ref.1, bf16[4,512,1024]{2,1,0:T(8,128)(2,1)} %get-tuple-element.19.dh_ref, bf16[4,512,512]{2,1,0:T(8,128)(2,1)} %get-tuple-element.20.a_ref, ...), custom_call_target="tpu_custom_call" | custom-call | flops 6442450944 | bytes 39845888 | tf_op jit(solution)/shard_map/weight_grads/pallas_call | solution.py:362
  61.5 0.0 collective-permute-done.left_ref
  61.5 0.0 collective-permute-done.1.right_ref
  61.5 0.0 copy-done
  61.5 0.8 %final_sum.1 = bf16[128,1024]{1,0:T(8,128)(2,1)} custom-call(f32[128,1024]{1,0:T(8,128)S(1)} %copy-done, f32[128,1024]{1,0:T(8,128)S(1)} %collective-permute-done.left_ref, f32[128,1024]{1,0:T(8,128)S(1)} %collective-permute-done.1.right_ref), custom_call_target="tpu_custom_call" | custom-call | tf_op jit(solution)/shard_map/final_sum/pallas_call | solution.py:396
Async XLA Ops:
  39.2 22.2 %collective-permute-start = (f32[128,1024]{1,0:T(8,128)}, f32[128,1024]{1,0:T(8,128)S(1)}, u32[]{:S(2)}, u32[]{:S(2)}) collective-permute-start(f32[128,1024]{1,0:T(8,128)} %get-tuple-element.17), channel_id=1, source_target_pairs={{0,2},{1,3},{2,4},{3,5},{4,6},{5,7},{6,0},{7,1},{8,10},{9,11},{10,... | collective-permute-start | bytes 1572872 | tf_op jit(solution)/shard_map/ppermute | solution.py:419
  40.1 21.4 %collective-permute-start.1 = (f32[128,1024]{1,0:T(8,128)}, f32[128,1024]{1,0:T(8,128)S(1)}, u32[]{:S(2)}, u32[]{:S(2)}) collective-permute-start(f32[128,1024]{1,0:T(8,128)} %get-tuple-element.18), channel_id=1, source_target_pairs={{0,6},{1,7},{2,0},{3,1},{4,2},{5,3},{6,4},{7,5},{8,14},{9,15},{10,... | collective-permute-start | bytes 1572872 | tf_op jit(solution)/shard_map/ppermute | solution.py:420
  42.0 19.5 %copy-start = (f32[128,1024]{1,0:T(8,128)S(1)}, f32[128,1024]{1,0:T(8,128)}, u32[]{:S(2)}) copy-start(f32[128,1024]{1,0:T(8,128)} %get-tuple-element.16.own_ref) | copy-start | bytes 1572868

commit v3 on v2

--- a/solution.py
+++ b/solution.py
@@ -9,6 +9,8 @@
 
 F32, BF16 = jnp.float32, jnp.bfloat16
 COLS = 256
+EXCHANGE_VMEM = 50 * 1024 * 1024
+WEIGHT_VMEM = 24 * 1024 * 1024
 OPP, LEFT, RIGHT, OWN = range(4)
 
 
@@ -21,10 +23,10 @@
 
 
 def exchange_kernel(axis, n_dev, topk_ref, slot_ref, gate_ref, count_ref, gy_hbm, y_hbm, hg_hbm, hu_hbm, wg_hbm, wu_hbm, wd_hbm,
-                    d_out, dh_out, a_out, gg_out, right_out, left_out, own_out,
-                    gy_all, route_send, route_all, y_buf, hg_buf, hu_buf, wgu_buf, wd_buf, f1_buf, s_buf, a_buf,
-                    oh_buf, d_buf, dh_buf, r_buf, keep_buf, pair_send, pair_recv, hop_recv,
-                    load_sem, store_sem, route_ssem, route_rsem, gy_ssem, gy_rsem, pair_ssem, pair_rsem, hop_ssem, hop_rsem):
+                    d_buf, dh_buf, a_buf, gg_out, right_out, left_out, own_out,
+                    gy_all, route_send, route_all, y_buf, hg_buf, hu_buf, wgu_buf, wd_buf, f1_buf, s_buf,
+                    oh_buf, r_buf, keep_buf, pair_send, pair_recv, hop_recv,
+                    load_sem, route_ssem, route_rsem, gy_ssem, gy_rsem, pair_ssem, pair_rsem, hop_ssem, hop_rsem):
     n_loc, n_rows, ffn = hg_hbm.shape
     tok, model = gy_hbm.shape
     top_k = topk_ref.shape[0]
@@ -144,8 +146,6 @@
 
     factors(2)
     factors(3)
-    store_a = pltpu.make_async_copy(a_buf, a_out, store_sem.at[4])
-    store_a.start()
 
     gy_wait(left, bottom, 1)
     gy_send(left, bottom, 8, sib)
@@ -216,19 +216,9 @@
         for n in range(0, model, COLS):
             dst[:, pl.ds(n, COLS)] = dot_first(pick, r_buf[s, :, pl.ds(n, COLS)])
 
-    stores = []
-
-    def store_rows(role):
-        rows = rows_of(chips[role])
-        for k, (src, dst) in enumerate(((d_buf, d_out), (dh_buf, dh_out))):
-            copy = pltpu.make_async_copy(src.at[:, rows], dst.at[:, rows], store_sem.at[5 + 2 * role + k])
-            copy.start()
-            stores.append(copy)
-
     pairs = {}
 
     def finish(role):
-        store_rows(role)
         sum_rows(others[role], pair_send.at[role])
         pairs[role] = remote(pair_send.at[role], pair_recv.at[role], pair_ssem.at[role], pair_rsem.at[role], sib)
         pairs[role].start()
@@ -285,9 +275,6 @@
 
     for copy in sends:
         copy.wait_send()
-    for copy in stores:
-        copy.wait()
-    store_a.wait()
 
 
 def exchange(axis, n_dev, topk_idx, slot_ids, gate_vals, pair_counts, grad_y, y_rows, h_gate, h_up, w_gate, w_up, w_down):
@@ -298,19 +285,19 @@
     vmem = pl.BlockSpec(memory_space=pltpu.VMEM)
     hbm = pl.BlockSpec(memory_space=pl.ANY)
     dma = pltpu.SemaphoreType.DMA
-    part = jax.ShapeDtypeStruct((tok, model), F32)
+    part = pltpu.VMEM((tok, model), F32)
     return pl.pallas_call(
         functools.partial(exchange_kernel, axis, n_dev),
         name="exchange",
         out_shape=(
-            jax.ShapeDtypeStruct((n_loc, n_rows, model), BF16),
-            jax.ShapeDtypeStruct((n_loc, n_rows, 2 * ffn), BF16),
-            jax.ShapeDtypeStruct((n_loc, n_rows, ffn), BF16),
-            jax.ShapeDtypeStruct((top_k, tok), F32),
+            pltpu.VMEM((n_loc, n_rows, model), BF16),
+            pltpu.VMEM((n_loc, n_rows, 2 * ffn), BF16),
+            pltpu.VMEM((n_loc, n_rows, ffn), BF16),
+            pltpu.VMEM((top_k, tok), F32),
             part, part, part,
         ),
         in_specs=[vmem] * 4 + [hbm] * 7,
-        out_specs=(hbm, hbm, hbm, vmem, vmem, vmem, vmem),
+        out_specs=(vmem,) * 7,
         scratch_shapes=[
             pltpu.VMEM((n_dev, tok, model), BF16),
             pltpu.VMEM((n_dev, 2 * n_loc, tok), F32),
@@ -322,69 +309,80 @@
             pltpu.VMEM(w_down.shape, BF16),
             pltpu.VMEM(h_gate.shape, F32),
             pltpu.VMEM(h_gate.shape, F32),
-            pltpu.VMEM(h_gate.shape, BF16),
             pltpu.VMEM((n_dev, n_loc * cap, tok), BF16),
-            pltpu.VMEM((n_loc, n_rows, model), BF16),
-            pltpu.VMEM((n_loc, n_rows, 2 * ffn), BF16),
             pltpu.VMEM((n_dev, n_loc * cap, model), BF16),
             pltpu.VMEM((4, tok, model), F32),
             pltpu.VMEM((4, tok, model), F32),
             pltpu.VMEM((4, tok, model), F32),
             pltpu.VMEM((2, tok // 2, model), F32),
-            dma((5 + 2 * n_loc,)), dma((13,)), dma((n_dev - 1,)), dma((n_dev - 1,)), dma((13,)), dma((13,)),
+            dma((5 + 2 * n_loc,)), dma((n_dev - 1,)), dma((n_dev - 1,)), dma((13,)), dma((13,)),
             dma((4,)), dma((4,)), dma((2,)), dma((2,)),
         ],
-        compiler_params=pltpu.CompilerParams(collective_id=0, has_side_effects=True, vmem_limit_bytes=60 * 1024 * 1024),
+        compiler_params=pltpu.CompilerParams(collective_id=0, has_side_effects=True, vmem_limit_bytes=EXCHANGE_VMEM),
     )(topk_idx, slot_ids, gate_vals, pair_counts, grad_y, y_rows, h_gate, h_up, w_gate, w_up, w_down)
 
 
-def weight_kernel(ffn, x_ref, dh_ref, a_ref, d_ref, gg_ref, wg_out, wu_out, wd_out, gg_out):
-    @pl.when((pl.program_id(0) == 0) & (pl.program_id(1) == 0))
-    def _():
-        gg_out[...] = gg_ref[...]
-
-    x = x_ref[0]
-    for n in range(0, ffn, COLS):
-        wg_out[0, :, pl.ds(n, COLS)] = dot_first(x, dh_ref[0, :, pl.ds(n, COLS)])
-        wu_out[0, :, pl.ds(n, COLS)] = dot_first(x, dh_ref[0, :, pl.ds(ffn + n, COLS)])
-    a = a_ref[0]
-    for n in range(0, d_ref.shape[2], COLS):
-        wd_out[0, :, pl.ds(n, COLS)] = dot_first(a, d_ref[0, :, pl.ds(n, COLS)])
+def weight_kernel(x_hbm, dh_buf, a_buf, d_buf, gg_ref, wg_hbm, wu_hbm, wd_hbm, gg_out, x_buf, wg_buf, wu_buf, wd_buf, in_sem, out_sem):
+    n_loc, ffn, model = a_buf.shape[0], a_buf.shape[2], d_buf.shape[2]
+    gg_out[...] = gg_ref[...]
+    ins = []
+    for e in range(n_loc):
+        ins.append(pltpu.make_async_copy(x_hbm.at[e], x_buf.at[e], in_sem.at[e]))
+        ins[e].start()
+    outs = {}
+
+    def store(key, src, dst, sem):
+        outs[key] = pltpu.make_async_copy(src, dst, sem)
+        outs[key].start()
+
+    for e in range(n_loc):
+        slot = e % 2
+        for k in range(3):
+            if (slot, k) in outs:
+                outs.pop((slot, k)).wait()
+        for n in range(0, model, COLS):
+            wd_buf[slot, :, pl.ds(n, COLS)] = dot_first(a_buf[e], d_buf[e, :, pl.ds(n, COLS)])
+        store((slot, 0), wd_buf.at[slot], wd_hbm.at[e], out_sem.at[slot, 0])
+        ins[e].wait()
+        for n in range(0, ffn, COLS):
+            wg_buf[slot, :, pl.ds(n, COLS)] = dot_first(x_buf[e], dh_buf[e, :, pl.ds(n, COLS)])
+        store((slot, 1), wg_buf.at[slot], wg_hbm.at[e], out_sem.at[slot, 1])
+        for n in range(0, ffn, COLS):
+            wu_buf[slot, :, pl.ds(n, COLS)] = dot_first(x_buf[e], dh_buf[e, :, pl.ds(ffn + n, COLS)])
+        store((slot, 2), wu_buf.at[slot], wu_hbm.at[e], out_sem.at[slot, 2])
+    for copy in outs.values():
+        copy.wait()
 
 
 def weight_grads(x_disp, dh_rows, a_rows, d_rows, gg):
     n_loc, n_rows, model = x_disp.shape
     ffn = a_rows.shape[2]
-    split = 2
-    m_blk, f_blk = model // split, ffn // split
     flops = 2 * n_loc * n_rows * model * 3 * ffn
-    moved = 2 * (x_disp.size + dh_rows.size + a_rows.size + d_rows.size) + 12 * n_loc * model * ffn
+    moved = 2 * x_disp.size + 12 * n_loc * model * ffn
+    vmem = pl.BlockSpec(memory_space=pltpu.VMEM)
+    hbm = pl.BlockSpec(memory_space=pl.ANY)
     return pl.pallas_call(
-        functools.partial(weight_kernel, ffn),
+        weight_kernel,
         name="weight_grads",
-        grid=(n_loc, split),
-        in_specs=[
-            pl.BlockSpec((1, n_rows, m_blk), lambda e, h: (e, 0, h)),
-            pl.BlockSpec((1, n_rows, 2 * ffn), lambda e, h: (e, 0, 0)),
-            pl.BlockSpec((1, n_rows, f_blk), lambda e, h: (e, 0, h)),
-            pl.BlockSpec((1, n_rows, model), lambda e, h: (e, 0, 0)),
-            pl.BlockSpec(gg.shape, lambda e, h: (0, 0)),
-        ],
-        out_specs=(
-            pl.BlockSpec((1, m_blk, ffn), lambda e, h: (e, h, 0)),
-            pl.BlockSpec((1, m_blk, ffn), lambda e, h: (e, h, 0)),
-            pl.BlockSpec((1, f_blk, model), lambda e, h: (e, h, 0)),
-            pl.BlockSpec(gg.shape, lambda e, h: (0, 0)),
-        ),
+        in_specs=[hbm] + [vmem] * 4,
+        out_specs=(hbm, hbm, hbm, vmem),
         out_shape=(
             jax.ShapeDtypeStruct((n_loc, model, ffn), F32),
             jax.ShapeDtypeStruct((n_loc, model, ffn), F32),
             jax.ShapeDtypeStruct((n_loc, ffn, model), F32),
             jax.ShapeDtypeStruct(gg.shape, F32),
         ),
+        scratch_shapes=[
+            pltpu.VMEM(x_disp.shape, BF16),
+            pltpu.VMEM((2, model, ffn), F32),
+            pltpu.VMEM((2, model, ffn), F32),
+            pltpu.VMEM((2, ffn, model), F32),
+            pltpu.SemaphoreType.DMA((n_loc,)),
+            pltpu.SemaphoreType.DMA((2, 3)),
+        ],
         cost_estimate=pl.CostEstimate(flops=flops, bytes_accessed=moved, transcendentals=0),
-        compiler_params=pltpu.CompilerParams(vmem_limit_bytes=60 * 1024 * 1024),
-    )(x_disp, dh_rows, a_rows, d_rows, gg)
+        compiler_params=pltpu.CompilerParams(vmem_limit_bytes=WEIGHT_VMEM),
+    )(pltpu.with_memory_space_constraint(x_disp, pltpu.HBM), *(pltpu.with_memory_space_constraint(rows, pltpu.VMEM) for rows in (dh_rows, a_rows, d_rows, gg)))
 
 
 def final_kernel(own_ref, left_ref, right_ref, gx_out):
@@ -400,7 +398,7 @@
         in_specs=[vmem] * 3,
         out_specs=vmem,
         compiler_params=pltpu.CompilerParams(vmem_limit_bytes=8 * 1024 * 1024),
-    )(own, from_left, from_right)
+    )(*(pltpu.with_memory_space_constraint(part, pltpu.VMEM) for part in (own, from_left, from_right)))
 
 
 def solution(mesh):

time: 62.5 us -> 53.1 us (0.85)
  Pallas kernels: 58.8 us -> 48.8 us
  waiting for transfers between devices: 0.01 us -> 0.73 us
    pallas_call x1, Pallas kernels: 19.4 us -> 10.7 us  [weight_grads(): pl.pallas_call(weight_kernel, name='weight_grads', in_specs=[hbm] + [vmem...]
    pallas_call x1, Pallas kernels: 38.6 us -> 37.3 us  [exchange(): pl.pallas_call(functools.partial(exchange_kernel, axis, n_dev), name='exc...]
    ppermute x1, waiting for transfers between devices: 0.01 us -> 0.73 us  [local_step(): from_left = lax.ppermute(for_right, axis, to_right)]
  transfers between devices with their start and end apart: 2 -> 2, of which waited for: 0 -> 1; matrix products, arithmetic and copies ran while one was open for 0% -> 0% of each run, Pallas kernels for 31% -> 20%
where the time goes in v3:
time: 53.1 us; the launch traced here: 53 us
  Pallas kernels  48.8 us (92%)
  starting transfers between devices  2.76 us (5%)
  waiting for transfers between devices  0.73 us (1%)
  between operations  0.65 us (1%)
    pallas_call x1, Pallas kernels, exchange(): pl.pallas_call(functools.partial(exchange_kernel, axis, n_dev), name='exc...  37.3 us
    pallas_call x1, Pallas kernels, weight_grads(): pl.pallas_call(weight_kernel, name='weight_grads', in_specs=[hbm] + [vmem...  10.7 us
    ppermute x1, starting transfers between devices, local_step(): from_right = lax.ppermute(for_left, axis, to_left)  1.94 us
  transfers between devices with their start and end apart: 2, of which 1 were waited for; matrix products, arithmetic and copies ran while one was open for 0% of the time, Pallas kernels for 20%

profile of v3, /device:TPU:81, one launch (start us, length us, event | category | flops | bytes accessed | tf_op | source)
XLA Modules:
  0.0 53.0 jit_solution(3173249098189423029)
XLA Ops:
  0.6 37.3 %exchange.1 = (bf16[4,512,1024]{2,1,0:T(8,128)(2,1)S(1)}, bf16[4,512,1024]{2,1,0:T(8,128)(2,1)S(1)}, bf16[4,512,512]{2,1,0:T(8,128)(2,1)S(1)}, f32[8,128]{1,0:T(...) custom-call(s32[8,128]{1,0:T(8,128)} %bitcast.6, s32[8,128]{1,0:T(8,128)} %bitcast.7, ...), custom_call_target="tpu_custom_call" | custom-call | tf_op jit(solution)/shard_map/exchange/pallas_call | solution.py:289
  38.0 0.8 %collective-permute-start = (f32[128,1024]{1,0:T(8,128)S(1)}, f32[128,1024]{1,0:T(8,128)S(1)}, u32[]{:S(2)}, u32[]{:S(2)}) collective-permute-start(f32[128,1024]{1,0:T(8,128)S(1)} %get-tuple-element.17), channel_id=1, source_target_pairs={{0,2},{1,3},{2,4},{3,5},{4,6},{5,7},{6,0},{7,1},{8,10},{9,11},{10,... | collective-permute-start | bytes 1572872 | tf_op jit(solution)/shard_map/ppermute | solution.py:417
  38.8 1.9 %collective-permute-start.1 = (f32[128,1024]{1,0:T(8,128)S(1)}, f32[128,1024]{1,0:T(8,128)S(1)}, u32[]{:S(2)}, u32[]{:S(2)}) collective-permute-start(f32[128,1024]{1,0:T(8,128)S(1)} %get-tuple-element.18), channel_id=1, source_target_pairs={{0,6},{1,7},{2,0},{3,1},{4,2},{5,3},{6,4},{7,5},{8,14},{9,15},{10,... | collective-permute-start | bytes 1572872 | tf_op jit(solution)/shard_map/ppermute | solution.py:418
  40.7 10.7 %weight_grads.1 = (f32[4,1024,512]{2,1,0:T(8,128)}, f32[4,1024,512]{2,1,0:T(8,128)}, f32[4,512,1024]{2,1,0:T(8,128)}, f32[8,128]{1,0:T(8,128)}) custom-call(bf16[4,512,1024]{2,1,0:T(8,128)(2,1)} %x_hbm.1, bf16[4,512,1024]{2,1,0:T(8,128)(2,1)S(1)} %get-tuple-element.19.dh_buf, bf16[4,512,512]{2,1,0:T(8,128)(2,1)S(1)} %get-tuple-element.20.a_buf, ...), custom_call_target="tpu_custom_call" | custom-call | flops 6442450944 | bytes 29360128 | tf_op jit(solution)/shard_map/weight_grads/pallas_call | solution.py:364
  51.5 0.7 %collective-permute-done.left_ref = f32[128,1024]{1,0:T(8,128)S(1)} collective-permute-done((f32[128,1024]{1,0:T(8,128)S(1)}, f32[128,1024]{1,0:T(8,128)S(1)}, u32[]{:S(2)}, u32[]{:S(2)}) %collective-permute-start) | collective-permute-done | bytes 524320 | tf_op jit(solution)/shard_map/ppermute | solution.py:417
  52.2 0.0 collective-permute-done.1.right_ref
  52.2 0.8 %final_sum.1 = bf16[128,1024]{1,0:T(8,128)(2,1)} custom-call(f32[128,1024]{1,0:T(8,128)S(1)} %get-tuple-element.16.own_ref, f32[128,1024]{1,0:T(8,128)S(1)} %collective-permute-done.left_ref, f32[128,1024]{1,0:T(8,128)S(1)} %collective-permute-done.1.right_ref), custom_call_target="tpu_custom_call" | custom-call | tf_op jit(solution)/shard_map/final_sum/pallas_call | solution.py:394
Async XLA Ops:
  38.0 14.2 %collective-permute-start = (f32[128,1024]{1,0:T(8,128)S(1)}, f32[128,1024]{1,0:T(8,128)S(1)}, u32[]{:S(2)}, u32[]{:S(2)}) collective-permute-start(f32[128,1024]{1,0:T(8,128)S(1)} %get-tuple-element.17), channel_id=1, source_target_pairs={{0,2},{1,3},{2,4},{3,5},{4,6},{5,7},{6,0},{7,1},{8,10},{9,11},{10,... | collective-permute-start | bytes 1572872 | tf_op jit(solution)/shard_map/ppermute | solution.py:417
  38.8 13.4 %collective-permute-start.1 = (f32[128,1024]{1,0:T(8,128)S(1)}, f32[128,1024]{1,0:T(8,128)S(1)}, u32[]{:S(2)}, u32[]{:S(2)}) collective-permute-start(f32[128,1024]{1,0:T(8,128)S(1)} %get-tuple-element.18), channel_id=1, source_target_pairs={{0,6},{1,7},{2,0},{3,1},{4,2},{5,3},{6,4},{7,5},{8,14},{9,15},{10,... | collective-permute-start | bytes 1572872 | tf_op jit(solution)/shard_map/ppermute | solution.py:418

commit v4 on v3

--- a/solution.py
+++ b/solution.py
@@ -25,7 +25,7 @@
 def exchange_kernel(axis, n_dev, topk_ref, slot_ref, gate_ref, count_ref, gy_hbm, y_hbm, hg_hbm, hu_hbm, wg_hbm, wu_hbm, wd_hbm,
                     d_buf, dh_buf, a_buf, gg_out, right_out, left_out, own_out,
                     gy_all, route_send, route_all, y_buf, hg_buf, hu_buf, wgu_buf, wd_buf, f1_buf, s_buf,
-                    oh_buf, r_buf, keep_buf, pair_send, pair_recv, hop_recv,
+                    oh_buf, r_buf, pair_send, pair_recv, opp_send, opp_keep, opp_recv, hop_recv,
                     load_sem, route_ssem, route_rsem, gy_ssem, gy_rsem, pair_ssem, pair_rsem, hop_ssem, hop_rsem):
     n_loc, n_rows, ffn = hg_hbm.shape
     tok, model = gy_hbm.shape
@@ -134,23 +134,8 @@
         loads[("hu", e)].wait()
         lax.fori_loop(0, n_chunk, body, 0)
 
-    factors(0)
-    factors(1)
-
-    gy_wait(left, top, 0)
-    gy_send(left, top, 4, right)
-    gy_send(left, top, 7, sib)
-    gy_wait(right, bottom, 2)
-    gy_send(right, bottom, 5, left)
-    gy_send(right, bottom, 9, sib)
-
-    factors(2)
-    factors(3)
-
-    gy_wait(left, bottom, 1)
-    gy_send(left, bottom, 8, sib)
-    gy_wait(right, top, 3)
-    gy_send(right, top, 10, sib)
+    for e in range(n_loc):
+        factors(e)
 
     loads["y"].wait()
     group = 32
@@ -165,11 +150,6 @@
     for step in range(1, n_dev):
         src = lax.rem(me + n_dev - step, n_dev)
         remote(route_send.at[src], route_all.at[src], route_ssem.at[step - 1], route_rsem.at[step - 1], src).wait_recv()
-
-    gy_wait(opp, top, 4)
-    gy_send(opp, top, 11, sib)
-    gy_wait(opp, bottom, 5)
-    gy_send(opp, bottom, 12, sib)
 
     slot_iota = lax.broadcasted_iota(jnp.int32, (cap, tok), 0).astype(F32)
 
@@ -190,7 +170,9 @@
     def rows_of(c):
         return pl.ds(pl.multiple_of(c * pair_rows, pair_rows), pair_rows)
 
-    def experts(which, lo, hi):
+    def hidden_grads(roles):
+        which = [chips[role] for role in roles]
+
         def body(e, carry):
             d_rows = jnp.concatenate([d_buf[e, rows_of(c)] for c in which], axis=0)
             for n in range(0, ffn, COLS):
@@ -199,9 +181,17 @@
                     part = grad[i * pair_rows : (i + 1) * pair_rows]
                     dh_buf[e, rows_of(c), pl.ds(n, COLS)] = (part * f1_buf[e, rows_of(c), pl.ds(n, COLS)]).astype(BF16)
                     dh_buf[e, rows_of(c), pl.ds(ffn + n, COLS)] = (part * s_buf[e, rows_of(c), pl.ds(n, COLS)]).astype(BF16)
+            return carry
+
+        lax.fori_loop(0, n_loc, body, 0)
+
+    def returned(roles, lo, hi, cols):
+        which = [chips[role] for role in roles]
+
+        def body(e, carry):
             dh_rows = jnp.concatenate([dh_buf[e, rows_of(c)] for c in which], axis=0)
             out_rows = pl.ds(pl.multiple_of(e * cap, cap), cap)
-            for n in range(0, model, COLS):
+            for n in cols:
                 ret = dot_last(dh_rows, wgu_buf[e, pl.ds(n, COLS)]).astype(BF16)
                 for i, c in enumerate(which):
                     for k in range(2):
@@ -211,67 +201,109 @@
 
         lax.fori_loop(lo, hi, body, 0)
 
-    def sum_rows(s, dst):
-        pick = oh_buf[s]
-        for n in range(0, model, COLS):
-            dst[:, pl.ds(n, COLS)] = dot_first(pick, r_buf[s, :, pl.ds(n, COLS)])
+    all_cols = range(0, model, COLS)
+
+    def token_sum(s, n):
+        return dot_first(oh_buf[s], r_buf[s, :, pl.ds(n, COLS)])
 
     pairs = {}
 
-    def finish(role):
-        sum_rows(others[role], pair_send.at[role])
-        pairs[role] = remote(pair_send.at[role], pair_recv.at[role], pair_ssem.at[role], pair_rsem.at[role], sib)
-        pairs[role].start()
-        sends.append(pairs[role])
-        sum_rows(homes[role], keep_buf.at[role])
+    def send_pair(key, slot, ref_send, ref_recv):
+        pairs[key] = remote(ref_send, ref_recv, pair_ssem.at[slot], pair_rsem.at[slot], sib)
+        pairs[key].start()
+        sends.append(pairs[key])
+
+    def finish(role, out):
+        for n in all_cols:
+            pair_send[role, :, pl.ds(n, COLS)] = token_sum(others[role], n)
+        send_pair(role, role, pair_send.at[role], pair_recv.at[role])
+        for n in all_cols:
+            out[:, pl.ds(n, COLS)] = token_sum(homes[role], n)
 
     loads["wd"].wait()
-    gy_wait(others[OPP], top, 11)
-    gy_wait(others[OPP], bottom, 12)
-    build_rows(homes[OPP])
-    build_rows(others[OPP])
-    loads["wg"].wait()
-    loads["wu"].wait()
-    experts([chips[OPP]], 0, n_loc)
-    finish(OPP)
-
-    gy_wait(others[LEFT], top, 7)
-    gy_wait(others[LEFT], bottom, 8)
-    gy_wait(others[RIGHT], bottom, 9)
-    gy_wait(others[RIGHT], top, 10)
-    for role in (LEFT, RIGHT):
-        build_rows(homes[role])
-        build_rows(others[role])
-    experts([chips[LEFT], chips[RIGHT]], 0, n_loc // 2)
-
-    pairs[OPP].wait_recv()
-    keep_buf[OPP] = keep_buf[OPP] + pair_recv[OPP]
-    hop_right = remote(keep_buf.at[OPP, top], hop_recv.at[0], hop_ssem.at[0], hop_rsem.at[0], right)
-    hop_right.start()
-    hop_left = remote(keep_buf.at[OPP, bottom], hop_recv.at[1], hop_ssem.at[1], hop_rsem.at[1], left)
-    hop_left.start()
-    sends.extend([hop_right, hop_left])
-
-    experts([chips[LEFT], chips[RIGHT]], n_loc // 2, n_loc)
-    finish(LEFT)
-    finish(RIGHT)
-
     gy_wait(others[OWN], pl.ds(0, tok), 6)
     build_rows(homes[OWN])
     build_rows(others[OWN])
-    experts([chips[OWN]], 0, n_loc)
-    finish(OWN)
-
+    hidden_grads([OWN])
+
+    gy_wait(left, top, 0)
+    gy_send(left, top, 4, right)
+    gy_send(left, top, 7, sib)
+    gy_wait(right, bottom, 2)
+    gy_send(right, bottom, 5, left)
+    gy_send(right, bottom, 9, sib)
+
+    loads["wg"].wait()
+    loads["wu"].wait()
+    returned([OWN], 0, n_loc - 1, all_cols)
+
+    gy_wait(left, bottom, 1)
+    gy_send(left, bottom, 8, sib)
+    gy_wait(right, top, 3)
+    gy_send(right, top, 10, sib)
+
+    returned([OWN], n_loc - 1, n_loc, all_cols)
+    finish(OWN, own_out)
+
+    build_rows(homes[LEFT])
+    build_rows(homes[RIGHT])
+    gy_wait(others[LEFT], top, 7)
+    gy_wait(others[LEFT], bottom, 8)
+    build_rows(others[LEFT])
+    gy_wait(others[RIGHT], bottom, 9)
+    gy_wait(others[RIGHT], top, 10)
+    build_rows(others[RIGHT])
+
+    gy_wait(opp, top, 4)
+    gy_send(opp, top, 11, sib)
+    gy_wait(opp, bottom, 5)
+    gy_send(opp, bottom, 12, sib)
+
+    hidden_grads([LEFT, RIGHT])
+
+    build_rows(homes[OPP])
+    gy_wait(others[OPP], top, 11)
+    gy_wait(others[OPP], bottom, 12)
+    build_rows(others[OPP])
+    hidden_grads([OPP])
+
+    hops = []
+
+    def hop(i):
+        pairs[OPP, i].wait_recv()
+        opp_keep[i] = opp_keep[i] + opp_recv[i]
+        for k, (part, dev) in enumerate(((top, right), (bottom, left))):
+            copy = remote(opp_keep.at[i, part], hop_recv.at[k, i], hop_ssem.at[k, i], hop_rsem.at[k, i], dev)
+            copy.start()
+            sends.append(copy)
+            hops.append((k, i, copy))
+
+    for i, n in enumerate(all_cols):
+        returned([OPP], 0, n_loc, [n])
+        opp_send[i] = token_sum(others[OPP], n)
+        send_pair((OPP, i), 4 + i, opp_send.at[i], opp_recv.at[i])
+        opp_keep[i] = token_sum(homes[OPP], n)
+        if i:
+            hop(i - 1)
+
+    half_loc = n_loc // 2
+    returned([LEFT, RIGHT], 0, half_loc, all_cols)
+    hop(model // COLS - 1)
+    returned([LEFT, RIGHT], half_loc, n_loc, all_cols)
+    finish(LEFT, left_out)
+    finish(RIGHT, right_out)
+
+    pairs[OWN].wait_recv()
+    own_out[...] = own_out[...] + pair_recv[OWN]
     pairs[LEFT].wait_recv()
+    left_out[...] = left_out[...] + pair_recv[LEFT]
     pairs[RIGHT].wait_recv()
-    right_out[bottom] = keep_buf[RIGHT, bottom] + pair_recv[RIGHT, bottom]
-    left_out[top] = keep_buf[LEFT, top] + pair_recv[LEFT, top]
-    pairs[OWN].wait_recv()
-    own_out[...] = keep_buf[OWN] + pair_recv[OWN]
-    hop_right.wait_recv()
-    right_out[top] = keep_buf[RIGHT, top] + pair_recv[RIGHT, top] + hop_recv[0]
-    hop_left.wait_recv()
-    left_out[bottom] = keep_buf[LEFT, bottom] + pair_recv[LEFT, bottom] + hop_recv[1]
+    right_out[...] = right_out[...] + pair_recv[RIGHT]
+    for k, i, copy in hops:
+        copy.wait_recv()
+        out, part = ((right_out, top), (left_out, bottom))[k]
+        cols = pl.ds(i * COLS, COLS)
+        out[part, cols] = out[part, cols] + hop_recv[k, i]
 
     for copy in sends:
         copy.wait_send()
@@ -313,10 +345,12 @@
             pltpu.VMEM((n_dev, n_loc * cap, model), BF16),
             pltpu.VMEM((4, tok, model), F32),
             pltpu.VMEM((4, tok, model), F32),
-            pltpu.VMEM((4, tok, model), F32),
-            pltpu.VMEM((2, tok // 2, model), F32),
+            pltpu.VMEM((model // COLS, tok, COLS), F32),
+            pltpu.VMEM((model // COLS, tok, COLS), F32),
+            pltpu.VMEM((model // COLS, tok, COLS), F32),
+            pltpu.VMEM((2, model // COLS, tok // 2, COLS), F32),
             dma((5 + 2 * n_loc,)), dma((n_dev - 1,)), dma((n_dev - 1,)), dma((13,)), dma((13,)),
-            dma((4,)), dma((4,)), dma((2,)), dma((2,)),
+            dma((4 + model // COLS,)), dma((4 + model // COLS,)), dma((2, model // COLS)), dma((2, model // COLS)),
         ],
         compiler_params=pltpu.CompilerParams(collective_id=0, has_side_effects=True, vmem_limit_bytes=EXCHANGE_VMEM),
     )(topk_idx, slot_ids, gate_vals, pair_counts, grad_y, y_rows, h_gate, h_up, w_gate, w_up, w_down)

time: 53.1 us -> 56 us (1.055)
  Pallas kernels: 48.8 us -> 51.1 us
  waiting for transfers between devices: 0.73 us -> 1.35 us
    pallas_call x1, Pallas kernels: 37.3 us -> 39.6 us  [exchange(): pl.pallas_call(functools.partial(exchange_kernel, axis, n_dev), name='exc...]
    ppermute x1, starting transfers between devices: 0.83 us -> 0.11 us  [local_step(): from_left = lax.ppermute(for_right, axis, to_right)]
    ppermute x1, starting transfers between devices: 1.94 us -> 2.65 us  [local_step(): from_right = lax.ppermute(for_left, axis, to_left)]
    ppermute x1, waiting for transfers between devices: 0.73 us -> 1.35 us  [local_step(): from_left = lax.ppermute(for_right, axis, to_right)]
  transfers between devices with their start and end apart: 2 -> 2, of which waited for: 1 -> 1; matrix products, arithmetic and copies ran while one was open for 0% -> 0% of each run, Pallas kernels for 20% -> 19%
where the time goes in v4:
time: 56 us; the launch traced here: 55.9 us
  Pallas kernels  51.1 us (91%)
  starting transfers between devices  2.76 us (5%)
  waiting for transfers between devices  1.35 us (2%)
  between operations  0.66 us (1%)
    pallas_call x1, Pallas kernels, exchange(): pl.pallas_call(functools.partial(exchange_kernel, axis, n_dev), name='exc...  39.6 us
    pallas_call x1, Pallas kernels, weight_grads(): pl.pallas_call(weight_kernel, name='weight_grads', in_specs=[hbm] + [vmem...  10.7 us
    ppermute x1, starting transfers between devices, local_step(): from_right = lax.ppermute(for_left, axis, to_left)  2.65 us
    ppermute x1, waiting for transfers between devices, local_step(): from_left = lax.ppermute(for_right, axis, to_right)  1.35 us
  transfers between devices with their start and end apart: 2, of which 1 were waited for; matrix products, arithmetic and copies ran while one was open for 0% of the time, Pallas kernels for 19%

profile of v4, /device:TPU:81, one launch (start us, length us, event | category | flops | bytes accessed | tf_op | source)
XLA Modules:
  0.0 55.9 jit_solution(8272945464849560696)
XLA Ops:
  0.6 39.6 %exchange.1 = (bf16[4,512,1024]{2,1,0:T(8,128)(2,1)S(1)}, bf16[4,512,1024]{2,1,0:T(8,128)(2,1)S(1)}, bf16[4,512,512]{2,1,0:T(8,128)(2,1)S(1)}, f32[8,128]{1,0:T(...) custom-call(s32[8,128]{1,0:T(8,128)} %bitcast.6, s32[8,128]{1,0:T(8,128)} %bitcast.7, ...), custom_call_target="tpu_custom_call" | custom-call | tf_op jit(solution)/shard_map/exchange/pallas_call | solution.py:321
  40.3 0.1 collective-permute-start
  40.4 2.7 %collective-permute-start.1 = (f32[128,1024]{1,0:T(8,128)S(1)}, f32[128,1024]{1,0:T(8,128)S(1)}, u32[]{:S(2)}, u32[]{:S(2)}) collective-permute-start(f32[128,1024]{1,0:T(8,128)S(1)} %get-tuple-element.18), channel_id=1, source_target_pairs={{0,6},{1,7},{2,0},{3,1},{4,2},{5,3},{6,4},{7,5},{8,14},{9,15},{10,... | collective-permute-start | bytes 1572872 | tf_op jit(solution)/shard_map/ppermute | solution.py:452
  43.0 10.7 %weight_grads.1 = (f32[4,1024,512]{2,1,0:T(8,128)}, f32[4,1024,512]{2,1,0:T(8,128)}, f32[4,512,1024]{2,1,0:T(8,128)}, f32[8,128]{1,0:T(8,128)}) custom-call(bf16[4,512,1024]{2,1,0:T(8,128)(2,1)} %x_hbm.1, bf16[4,512,1024]{2,1,0:T(8,128)(2,1)S(1)} %get-tuple-element.19.dh_buf, bf16[4,512,512]{2,1,0:T(8,128)(2,1)S(1)} %get-tuple-element.20.a_buf, ...), custom_call_target="tpu_custom_call" | custom-call | flops 6442450944 | bytes 29360128 | tf_op jit(solution)/shard_map/weight_grads/pallas_call | solution.py:398
  53.8 1.3 %collective-permute-done.left_ref = f32[128,1024]{1,0:T(8,128)S(1)} collective-permute-done((f32[128,1024]{1,0:T(8,128)S(1)}, f32[128,1024]{1,0:T(8,128)S(1)}, u32[]{:S(2)}, u32[]{:S(2)}) %collective-permute-start) | collective-permute-done | bytes 524320 | tf_op jit(solution)/shard_map/ppermute | solution.py:451
  55.1 0.0 collective-permute-done.1.right_ref
  55.1 0.8 %final_sum.1 = bf16[128,1024]{1,0:T(8,128)(2,1)} custom-call(f32[128,1024]{1,0:T(8,128)S(1)} %get-tuple-element.16.own_ref, f32[128,1024]{1,0:T(8,128)S(1)} %collective-permute-done.left_ref, f32[128,1024]{1,0:T(8,128)S(1)} %collective-permute-done.1.right_ref), custom_call_target="tpu_custom_call" | custom-call | tf_op jit(solution)/shard_map/final_sum/pallas_call | solution.py:428
Async XLA Ops:
  40.3 14.8 %collective-permute-start = (f32[128,1024]{1,0:T(8,128)S(1)}, f32[128,1024]{1,0:T(8,128)S(1)}, u32[]{:S(2)}, u32[]{:S(2)}) collective-permute-start(f32[128,1024]{1,0:T(8,128)S(1)} %get-tuple-element.17), channel_id=1, source_target_pairs={{0,2},{1,3},{2,4},{3,5},{4,6},{5,7},{6,0},{7,1},{8,10},{9,11},{10,... | collective-permute-start | bytes 1572872 | tf_op jit(solution)/shard_map/ppermute | solution.py:451
  40.4 14.7 %collective-permute-start.1 = (f32[128,1024]{1,0:T(8,128)S(1)}, f32[128,1024]{1,0:T(8,128)S(1)}, u32[]{:S(2)}, u32[]{:S(2)}) collective-permute-start(f32[128,1024]{1,0:T(8,128)S(1)} %get-tuple-element.18), channel_id=1, source_target_pairs={{0,6},{1,7},{2,0},{3,1},{4,2},{5,3},{6,4},{7,5},{8,14},{9,15},{10,... | collective-permute-start | bytes 1572872 | tf_op jit(solution)/shard_map/ppermute | solution.py:452

commit v5 on v4

--- a/solution.py
+++ b/solution.py
@@ -64,6 +64,30 @@
     load("wd", wd_hbm, wd_buf)
     load("wg", wg_hbm, wgu_buf.at[:, :, pl.ds(0, ffn)])
     load("wu", wu_hbm, wgu_buf.at[:, :, pl.ds(ffn, ffn)])
+
+    loads["gy"].wait()
+    pl.semaphore_wait(barrier, n_dev - 1)
+
+    def remote(src, dst, ssem, rsem, dev):
+        return pltpu.make_async_remote_copy(src_ref=src, dst_ref=dst, send_sem=ssem, recv_sem=rsem, device_id={axis: dev}, device_id_type=pl.DeviceIdType.MESH)
+
+    sends = []
+
+    def gy_copy(block, part, send_slot, recv_slot, dev):
+        ref = gy_all.at[block, part]
+        return remote(ref, ref, gy_ssem.at[send_slot], gy_rsem.at[recv_slot], dev)
+
+    def gy_send(block, part, recv_slot, dev):
+        copy = gy_copy(block, part, recv_slot, recv_slot, dev)
+        copy.start()
+        sends.append(copy)
+
+    def gy_wait(block, part, recv_slot):
+        gy_copy(block, part, recv_slot, recv_slot, sib).wait_recv()
+
+    gy_send(me, top, 0, right)
+    gy_send(me, bottom, 2, left)
+    gy_send(me, pl.ds(0, tok), 6, sib)
 
     topk_t = topk_ref[...].astype(F32)
     slot_t = slot_ref[...].astype(F32)
@@ -84,36 +108,14 @@
         route_send[i, n_loc : 2 * n_loc] = gate_d[i * n_loc : (i + 1) * n_loc]
     route_all[me] = route_send[me]
 
-    loads["gy"].wait()
-    pl.semaphore_wait(barrier, n_dev - 1)
-
-    def remote(src, dst, ssem, rsem, dev):
-        return pltpu.make_async_remote_copy(src_ref=src, dst_ref=dst, send_sem=ssem, recv_sem=rsem, device_id={axis: dev}, device_id_type=pl.DeviceIdType.MESH)
-
-    sends = []
-
-    def gy_copy(block, part, send_slot, recv_slot, dev):
-        ref = gy_all.at[block, part]
-        return remote(ref, ref, gy_ssem.at[send_slot], gy_rsem.at[recv_slot], dev)
-
-    def gy_send(block, part, recv_slot, dev):
-        copy = gy_copy(block, part, recv_slot, recv_slot, dev)
+    peers = [sib, left, others[LEFT], right, others[RIGHT], opp, others[OPP]]
+    arrives = [0, 3, 4, 1, 2, 5, 6]
+    for k, dst in enumerate(peers):
+        copy = remote(route_send.at[dst], route_all.at[me], route_ssem.at[k], route_rsem.at[arrives[k]], dst)
         copy.start()
         sends.append(copy)
-
-    def gy_wait(block, part, recv_slot):
-        gy_copy(block, part, recv_slot, recv_slot, sib).wait_recv()
-
-    gy_send(me, top, 0, right)
-    gy_send(me, bottom, 2, left)
     gy_send(me, bottom, 1, right)
     gy_send(me, top, 3, left)
-    gy_send(me, pl.ds(0, tok), 6, sib)
-    for step in range(1, n_dev):
-        dst = lax.rem(me + step, n_dev)
-        copy = remote(route_send.at[dst], route_all.at[me], route_ssem.at[step - 1], route_rsem.at[step - 1], dst)
-        copy.start()
-        sends.append(copy)
 
     chunk = 32
     n_chunk = n_rows // chunk
@@ -137,19 +139,9 @@
     for e in range(n_loc):
         factors(e)
 
-    loads["y"].wait()
-    group = 32
-    gg = jnp.zeros((top_k, tok), F32)
-    tok_major = lax.broadcasted_iota(jnp.int32, (group, top_k, tok), 0)
-    tok_lane = lax.broadcasted_iota(jnp.int32, (group, top_k, tok), 2)
-    for i in range(tok // group):
-        prod = dot_last(y_buf[pl.ds(i * group * top_k, group * top_k)], gy_all[me])
-        gg += jnp.sum(jnp.where(tok_major + i * group == tok_lane, prod.reshape(group, top_k, tok), 0.0), axis=0)
-    gg_out[...] = gg
-
-    for step in range(1, n_dev):
-        src = lax.rem(me + n_dev - step, n_dev)
-        remote(route_send.at[src], route_all.at[src], route_ssem.at[step - 1], route_rsem.at[step - 1], src).wait_recv()
+    def route_wait(*slots):
+        for k in slots:
+            remote(route_send.at[peers[k]], route_all.at[peers[k]], route_ssem.at[k], route_rsem.at[k], peers[k]).wait_recv()
 
     slot_iota = lax.broadcasted_iota(jnp.int32, (cap, tok), 0).astype(F32)
 
@@ -183,7 +175,7 @@
                     dh_buf[e, rows_of(c), pl.ds(ffn + n, COLS)] = (part * s_buf[e, rows_of(c), pl.ds(n, COLS)]).astype(BF16)
             return carry
 
-        lax.fori_loop(0, n_loc, body, 0)
+        lax.fori_loop(0, n_loc, body, 0, unroll=True)
 
     def returned(roles, lo, hi, cols):
         which = [chips[role] for role in roles]
@@ -199,7 +191,7 @@
                         r_buf[2 * c + k, out_rows, pl.ds(n, COLS)] = ret[lo_row : lo_row + cap]
             return carry
 
-        lax.fori_loop(lo, hi, body, 0)
+        lax.fori_loop(lo, hi, body, 0, unroll=True)
 
     all_cols = range(0, model, COLS)
 
@@ -213,14 +205,17 @@
         pairs[key].start()
         sends.append(pairs[key])
 
-    def finish(role, out):
-        for n in all_cols:
-            pair_send[role, :, pl.ds(n, COLS)] = token_sum(others[role], n)
-        send_pair(role, role, pair_send.at[role], pair_recv.at[role])
-        for n in all_cols:
-            out[:, pl.ds(n, COLS)] = token_sum(homes[role], n)
+    def finish(*roles):
+        for role, _ in roles:
+            for n in all_cols:
+                pair_send[role, :, pl.ds(n, COLS)] = token_sum(others[role], n)
+            send_pair(role, role, pair_send.at[role], pair_recv.at[role])
+        for role, out in roles:
+            for n in all_cols:
+                out[:, pl.ds(n, COLS)] = token_sum(homes[role], n)
 
     loads["wd"].wait()
+    route_wait(0)
     gy_wait(others[OWN], pl.ds(0, tok), 6)
     build_rows(homes[OWN])
     build_rows(others[OWN])
@@ -235,16 +230,16 @@
 
     loads["wg"].wait()
     loads["wu"].wait()
-    returned([OWN], 0, n_loc - 1, all_cols)
+    returned([OWN], 0, n_loc, all_cols)
 
     gy_wait(left, bottom, 1)
     gy_send(left, bottom, 8, sib)
     gy_wait(right, top, 3)
     gy_send(right, top, 10, sib)
 
-    returned([OWN], n_loc - 1, n_loc, all_cols)
-    finish(OWN, own_out)
-
+    finish((OWN, own_out))
+
+    route_wait(1, 2, 3, 4)
     build_rows(homes[LEFT])
     build_rows(homes[RIGHT])
     gy_wait(others[LEFT], top, 7)
@@ -260,6 +255,7 @@
     gy_send(opp, bottom, 12, sib)
 
     hidden_grads([LEFT, RIGHT])
+    route_wait(5, 6)
 
     build_rows(homes[OPP])
     gy_wait(others[OPP], top, 11)
@@ -290,8 +286,17 @@
     returned([LEFT, RIGHT], 0, half_loc, all_cols)
     hop(model // COLS - 1)
     returned([LEFT, RIGHT], half_loc, n_loc, all_cols)
-    finish(LEFT, left_out)
-    finish(RIGHT, right_out)
+    finish((LEFT, left_out), (RIGHT, right_out))
+
+    loads["y"].wait()
+    group = 32
+    gg = jnp.zeros((top_k, tok), F32)
+    tok_major = lax.broadcasted_iota(jnp.int32, (group, top_k, tok), 0)
+    tok_lane = lax.broadcasted_iota(jnp.int32, (group, top_k, tok), 2)
+    for i in range(tok // group):
+        prod = dot_last(y_buf[pl.ds(i * group * top_k, group * top_k)], gy_all[me])
+        gg += jnp.sum(jnp.where(tok_major + i * group == tok_lane, prod.reshape(group, top_k, tok), 0.0), axis=0)
+    gg_out[...] = gg
 
     pairs[OWN].wait_recv()
     own_out[...] = own_out[...] + pair_recv[OWN]

time: 56 us -> 46.5 us (0.83)
  Pallas kernels: 51.1 us -> 42.3 us
  waiting for transfers between devices: 1.35 us -> 0.58 us
    pallas_call x1, Pallas kernels: 39.6 us -> 30.8 us  [exchange(): pl.pallas_call(functools.partial(exchange_kernel, axis, n_dev), name='exc...]
    ppermute x1, waiting for transfers between devices: 1.35 us -> 0.57 us  [local_step(): from_left = lax.ppermute(for_right, axis, to_right)]
  transfers between devices with their start and end apart: 2 -> 2, of which waited for: 1 -> 1; matrix products, arithmetic and copies ran while one was open for 0% -> 0% of each run, Pallas kernels for 19% -> 23%
where the time goes in v5:
time: 46.5 us; the launch traced here: 46.3 us
  Pallas kernels  42.3 us (91%)
  starting transfers between devices  2.76 us (6%)
  between operations  0.65 us (1%)
  waiting for transfers between devices  0.58 us (1%)
    pallas_call x1, Pallas kernels, exchange(): pl.pallas_call(functools.partial(exchange_kernel, axis, n_dev), name='exc...  30.8 us
    pallas_call x1, Pallas kernels, weight_grads(): pl.pallas_call(weight_kernel, name='weight_grads', in_specs=[hbm] + [vmem...  10.7 us
    ppermute x1, starting transfers between devices, local_step(): from_right = lax.ppermute(for_left, axis, to_left)  2.45 us
  transfers between devices with their start and end apart: 2, of which 1 were waited for; matrix products, arithmetic and copies ran while one was open for 0% of the time, Pallas kernels for 23%

profile of v5, /device:TPU:81, one launch (start us, length us, event | category | flops | bytes accessed | tf_op | source)
XLA Modules:
  0.0 46.3 jit_solution(13947391023471663649)
XLA Ops:
  0.6 30.8 %exchange.1 = (bf16[4,512,1024]{2,1,0:T(8,128)(2,1)S(1)}, bf16[4,512,1024]{2,1,0:T(8,128)(2,1)S(1)}, bf16[4,512,512]{2,1,0:T(8,128)(2,1)S(1)}, f32[8,128]{1,0:T(...) custom-call(s32[8,128]{1,0:T(8,128)} %bitcast.6, s32[8,128]{1,0:T(8,128)} %bitcast.7, ...), custom_call_target="tpu_custom_call" | custom-call | tf_op jit(solution)/shard_map/exchange/pallas_call | solution.py:326
  31.4 0.3 collective-permute-start
  31.8 2.4 %collective-permute-start.1 = (f32[128,1024]{1,0:T(8,128)S(1)}, f32[128,1024]{1,0:T(8,128)S(1)}, u32[]{:S(2)}, u32[]{:S(2)}) collective-permute-start(f32[128,1024]{1,0:T(8,128)S(1)} %get-tuple-element.18), channel_id=1, source_target_pairs={{0,6},{1,7},{2,0},{3,1},{4,2},{5,3},{6,4},{7,5},{8,14},{9,15},{10,... | collective-permute-start | bytes 1572872 | tf_op jit(solution)/shard_map/ppermute | solution.py:457
  34.2 10.7 %weight_grads.1 = (f32[4,1024,512]{2,1,0:T(8,128)}, f32[4,1024,512]{2,1,0:T(8,128)}, f32[4,512,1024]{2,1,0:T(8,128)}, f32[8,128]{1,0:T(8,128)}) custom-call(bf16[4,512,1024]{2,1,0:T(8,128)(2,1)} %x_hbm.1, bf16[4,512,1024]{2,1,0:T(8,128)(2,1)S(1)} %get-tuple-element.19.dh_buf, bf16[4,512,512]{2,1,0:T(8,128)(2,1)S(1)} %get-tuple-element.20.a_buf, ...), custom_call_target="tpu_custom_call" | custom-call | flops 6442450944 | bytes 29360128 | tf_op jit(solution)/shard_map/weight_grads/pallas_call | solution.py:403
  44.9 0.6 %collective-permute-done.left_ref = f32[128,1024]{1,0:T(8,128)S(1)} collective-permute-done((f32[128,1024]{1,0:T(8,128)S(1)}, f32[128,1024]{1,0:T(8,128)S(1)}, u32[]{:S(2)}, u32[]{:S(2)}) %collective-permute-start) | collective-permute-done | bytes 524320 | tf_op jit(solution)/shard_map/ppermute | solution.py:456
  45.5 0.0 collective-permute-done.1.right_ref
  45.5 0.8 %final_sum.1 = bf16[128,1024]{1,0:T(8,128)(2,1)} custom-call(f32[128,1024]{1,0:T(8,128)S(1)} %get-tuple-element.16.own_ref, f32[128,1024]{1,0:T(8,128)S(1)} %collective-permute-done.left_ref, f32[128,1024]{1,0:T(8,128)S(1)} %collective-permute-done.1.right_ref), custom_call_target="tpu_custom_call" | custom-call | tf_op jit(solution)/shard_map/final_sum/pallas_call | solution.py:433
Async XLA Ops:
  31.4 14.1 %collective-permute-start = (f32[128,1024]{1,0:T(8,128)S(1)}, f32[128,1024]{1,0:T(8,128)S(1)}, u32[]{:S(2)}, u32[]{:S(2)}) collective-permute-start(f32[128,1024]{1,0:T(8,128)S(1)} %get-tuple-element.17), channel_id=1, source_target_pairs={{0,2},{1,3},{2,4},{3,5},{4,6},{5,7},{6,0},{7,1},{8,10},{9,11},{10,... | collective-permute-start | bytes 1572872 | tf_op jit(solution)/shard_map/ppermute | solution.py:456
  31.8 13.8 %collective-permute-start.1 = (f32[128,1024]{1,0:T(8,128)S(1)}, f32[128,1024]{1,0:T(8,128)S(1)}, u32[]{:S(2)}, u32[]{:S(2)}) collective-permute-start(f32[128,1024]{1,0:T(8,128)S(1)} %get-tuple-element.18), channel_id=1, source_target_pairs={{0,6},{1,7},{2,0},{3,1},{4,2},{5,3},{6,4},{7,5},{8,14},{9,15},{10,... | collective-permute-start | bytes 1572872 | tf_op jit(solution)/shard_map/ppermute | solution.py:457

commit v6 on v5

--- a/solution.py
+++ b/solution.py
@@ -9,7 +9,7 @@
 
 F32, BF16 = jnp.float32, jnp.bfloat16
 COLS = 256
-EXCHANGE_VMEM = 50 * 1024 * 1024
+EXCHANGE_VMEM = 51 * 1024 * 1024
 WEIGHT_VMEM = 24 * 1024 * 1024
 OPP, LEFT, RIGHT, OWN = range(4)
 
@@ -24,7 +24,7 @@
 
 def exchange_kernel(axis, n_dev, topk_ref, slot_ref, gate_ref, count_ref, gy_hbm, y_hbm, hg_hbm, hu_hbm, wg_hbm, wu_hbm, wd_hbm,
                     d_buf, dh_buf, a_buf, gg_out, right_out, left_out, own_out,
-                    gy_all, route_send, route_all, y_buf, hg_buf, hu_buf, wgu_buf, wd_buf, f1_buf, s_buf,
+                    gy_all, route_send, route_all, y_buf, hg_buf, hu_buf, wgu_buf, wd_buf, wgu_turned, wd_turned, f1_buf, s_buf,
                     oh_buf, r_buf, pair_send, pair_recv, opp_send, opp_keep, opp_recv, hop_recv,
                     load_sem, route_ssem, route_rsem, gy_ssem, gy_rsem, pair_ssem, pair_rsem, hop_ssem, hop_rsem):
     n_loc, n_rows, ffn = hg_hbm.shape
@@ -44,7 +44,8 @@
     others = [2 * c + 1 - core for c in chips]
     opp, left, right = homes[OPP], homes[LEFT], homes[RIGHT]
     sib = others[OWN]
-    top, bottom = pl.ds(0, half), pl.ds(half, half)
+    top, bottom, whole = pl.ds(0, half), pl.ds(half, half), pl.ds(0, tok)
+    quarter = [pl.ds(i * (tok // 4), tok // 4) for i in range(4)]
 
     barrier = pltpu.get_barrier_semaphore()
     for step in range(1, n_dev):
@@ -60,10 +61,10 @@
     for e in range(n_loc):
         load(("hg", e), hg_hbm.at[e], hg_buf.at[e])
         load(("hu", e), hu_hbm.at[e], hu_buf.at[e])
-    load("y", y_hbm, y_buf)
     load("wd", wd_hbm, wd_buf)
     load("wg", wg_hbm, wgu_buf.at[:, :, pl.ds(0, ffn)])
     load("wu", wu_hbm, wgu_buf.at[:, :, pl.ds(ffn, ffn)])
+    load("y", y_hbm, y_buf)
 
     loads["gy"].wait()
     pl.semaphore_wait(barrier, n_dev - 1)
@@ -85,9 +86,11 @@
     def gy_wait(block, part, recv_slot):
         gy_copy(block, part, recv_slot, recv_slot, sib).wait_recv()
 
-    gy_send(me, top, 0, right)
-    gy_send(me, bottom, 2, left)
-    gy_send(me, pl.ds(0, tok), 6, sib)
+    gy_send(me, quarter[0], 0, right)
+    gy_send(me, quarter[2], 4, left)
+    gy_send(me, quarter[1], 1, right)
+    gy_send(me, quarter[3], 5, left)
+    gy_send(me, whole, 12, sib)
 
     topk_t = topk_ref[...].astype(F32)
     slot_t = slot_ref[...].astype(F32)
@@ -114,8 +117,8 @@
         copy = remote(route_send.at[dst], route_all.at[me], route_ssem.at[k], route_rsem.at[arrives[k]], dst)
         copy.start()
         sends.append(copy)
-    gy_send(me, bottom, 1, right)
-    gy_send(me, top, 3, left)
+    gy_send(me, quarter[2], 2, right)
+    gy_send(me, quarter[0], 6, left)
 
     chunk = 32
     n_chunk = n_rows // chunk
@@ -162,20 +165,31 @@
     def rows_of(c):
         return pl.ds(pl.multiple_of(c * pair_rows, pair_rows), pair_rows)
 
-    def hidden_grads(roles):
+    def turn(src, dst, e):
+        for i in range(0, src.shape[1], COLS):
+            for j in range(0, src.shape[2], COLS):
+                dst[e, pl.ds(j, COLS), pl.ds(i, COLS)] = src[e, pl.ds(i, COLS), pl.ds(j, COLS)].T
+
+    def hidden_grads(roles, lo, hi):
         which = [chips[role] for role in roles]
 
         def body(e, carry):
             d_rows = jnp.concatenate([d_buf[e, rows_of(c)] for c in which], axis=0)
             for n in range(0, ffn, COLS):
-                grad = dot_last(d_rows, wd_buf[e, pl.ds(n, COLS)]).astype(BF16).astype(F32)
+                if roles == [OWN]:
+                    grad = dot_last(d_rows, wd_buf[e, pl.ds(n, COLS)])
+                else:
+                    grad = jnp.dot(d_rows, wd_turned[e, :, pl.ds(n, COLS)], preferred_element_type=F32)
+                grad = grad.astype(BF16).astype(F32)
                 for i, c in enumerate(which):
                     part = grad[i * pair_rows : (i + 1) * pair_rows]
                     dh_buf[e, rows_of(c), pl.ds(n, COLS)] = (part * f1_buf[e, rows_of(c), pl.ds(n, COLS)]).astype(BF16)
                     dh_buf[e, rows_of(c), pl.ds(ffn + n, COLS)] = (part * s_buf[e, rows_of(c), pl.ds(n, COLS)]).astype(BF16)
+            if roles == [OWN]:
+                turn(wd_buf, wd_turned, e)
             return carry
 
-        lax.fori_loop(0, n_loc, body, 0, unroll=True)
+        lax.fori_loop(lo, hi, body, 0, unroll=True)
 
     def returned(roles, lo, hi, cols):
         which = [chips[role] for role in roles]
@@ -184,19 +198,25 @@
             dh_rows = jnp.concatenate([dh_buf[e, rows_of(c)] for c in which], axis=0)
             out_rows = pl.ds(pl.multiple_of(e * cap, cap), cap)
             for n in cols:
-                ret = dot_last(dh_rows, wgu_buf[e, pl.ds(n, COLS)]).astype(BF16)
-                for i, c in enumerate(which):
+                if roles == [OWN]:
+                    ret = dot_last(dh_rows, wgu_buf[e, pl.ds(n, COLS)])
+                else:
+                    ret = jnp.dot(dh_rows, wgu_turned[e, :, pl.ds(n, COLS)], preferred_element_type=F32)
+                ret = ret.astype(BF16)
+                for i in range(len(which)):
                     for k in range(2):
                         lo_row = i * pair_rows + k * cap
-                        r_buf[2 * c + k, out_rows, pl.ds(n, COLS)] = ret[lo_row : lo_row + cap]
+                        r_buf[2 * i + k, out_rows, pl.ds(n, COLS)] = ret[lo_row : lo_row + cap]
+            if roles == [OWN]:
+                turn(wgu_buf, wgu_turned, e)
             return carry
 
         lax.fori_loop(lo, hi, body, 0, unroll=True)
 
     all_cols = range(0, model, COLS)
 
-    def token_sum(s, n):
-        return dot_first(oh_buf[s], r_buf[s, :, pl.ds(n, COLS)])
+    def token_sum(role, k, n):
+        return dot_first(oh_buf[2 * chips[role] + k], r_buf[2 * (role == RIGHT) + k, :, pl.ds(n, COLS)])
 
     pairs = {}
 
@@ -205,88 +225,47 @@
         pairs[key].start()
         sends.append(pairs[key])
 
-    def finish(*roles):
+    def finish(cols, part, *roles):
         for role, _ in roles:
-            for n in all_cols:
-                pair_send[role, :, pl.ds(n, COLS)] = token_sum(others[role], n)
-            send_pair(role, role, pair_send.at[role], pair_recv.at[role])
+            for n in cols:
+                pair_send[role - 1, :, pl.ds(n, COLS)] = token_sum(role, 1 - core, n)
+            block = pl.ds(cols[0], len(cols) * COLS)
+            send_pair((role, part), 2 * (role - 1) + part, pair_send.at[role - 1, :, block], pair_recv.at[role - 1, :, block])
         for role, out in roles:
-            for n in all_cols:
-                out[:, pl.ds(n, COLS)] = token_sum(homes[role], n)
+            for n in cols:
+                out[:, pl.ds(n, COLS)] = token_sum(role, core, n)
+
+    def add_pair(role, part, cols, out):
+        pairs[role, part].wait_recv()
+        block = pl.ds(cols[0], len(cols) * COLS)
+        out[:, block] = out[:, block] + pair_recv[role - 1, :, block]
 
     loads["wd"].wait()
     route_wait(0)
-    gy_wait(others[OWN], pl.ds(0, tok), 6)
+    gy_wait(others[OWN], whole, 12)
     build_rows(homes[OWN])
     build_rows(others[OWN])
-    hidden_grads([OWN])
-
-    gy_wait(left, top, 0)
-    gy_send(left, top, 4, right)
-    gy_send(left, top, 7, sib)
-    gy_wait(right, bottom, 2)
-    gy_send(right, bottom, 5, left)
-    gy_send(right, bottom, 9, sib)
-
+    hidden_grads([OWN], 0, n_loc - 1)
+    gy_wait(left, quarter[0], 0)
+    gy_send(left, quarter[0], 8, right)
+    gy_wait(right, quarter[2], 4)
+    gy_send(right, quarter[2], 10, left)
+
+    hidden_grads([OWN], n_loc - 1, n_loc)
     loads["wg"].wait()
     loads["wu"].wait()
-    returned([OWN], 0, n_loc, all_cols)
-
-    gy_wait(left, bottom, 1)
-    gy_send(left, bottom, 8, sib)
-    gy_wait(right, top, 3)
-    gy_send(right, top, 10, sib)
-
-    finish((OWN, own_out))
-
-    route_wait(1, 2, 3, 4)
-    build_rows(homes[LEFT])
-    build_rows(homes[RIGHT])
-    gy_wait(others[LEFT], top, 7)
-    gy_wait(others[LEFT], bottom, 8)
-    build_rows(others[LEFT])
-    gy_wait(others[RIGHT], bottom, 9)
-    gy_wait(others[RIGHT], top, 10)
-    build_rows(others[RIGHT])
-
-    gy_wait(opp, top, 4)
-    gy_send(opp, top, 11, sib)
-    gy_wait(opp, bottom, 5)
-    gy_send(opp, bottom, 12, sib)
-
-    hidden_grads([LEFT, RIGHT])
-    route_wait(5, 6)
-
-    build_rows(homes[OPP])
-    gy_wait(others[OPP], top, 11)
-    gy_wait(others[OPP], bottom, 12)
-    build_rows(others[OPP])
-    hidden_grads([OPP])
-
-    hops = []
-
-    def hop(i):
-        pairs[OPP, i].wait_recv()
-        opp_keep[i] = opp_keep[i] + opp_recv[i]
-        for k, (part, dev) in enumerate(((top, right), (bottom, left))):
-            copy = remote(opp_keep.at[i, part], hop_recv.at[k, i], hop_ssem.at[k, i], hop_rsem.at[k, i], dev)
-            copy.start()
-            sends.append(copy)
-            hops.append((k, i, copy))
-
-    for i, n in enumerate(all_cols):
-        returned([OPP], 0, n_loc, [n])
-        opp_send[i] = token_sum(others[OPP], n)
-        send_pair((OPP, i), 4 + i, opp_send.at[i], opp_recv.at[i])
-        opp_keep[i] = token_sum(homes[OPP], n)
-        if i:
-            hop(i - 1)
-
-    half_loc = n_loc // 2
-    returned([LEFT, RIGHT], 0, half_loc, all_cols)
-    hop(model // COLS - 1)
-    returned([LEFT, RIGHT], half_loc, n_loc, all_cols)
-    finish((LEFT, left_out), (RIGHT, right_out))
+    returned([OWN], 0, 1, all_cols)
+
+    gy_wait(left, quarter[1], 1)
+    gy_send(left, quarter[1], 9, right)
+    gy_send(me, quarter[3], 3, right)
+    gy_wait(right, quarter[3], 5)
+    gy_send(right, quarter[3], 11, left)
+    gy_send(me, quarter[1], 7, left)
+    gy_send(left, top, 13, sib)
+    gy_send(right, bottom, 15, sib)
+    returned([OWN], 1, n_loc, all_cols)
+    finish(all_cols, 0, (OWN, own_out))
 
     loads["y"].wait()
     group = 32
@@ -298,12 +277,66 @@
         gg += jnp.sum(jnp.where(tok_major + i * group == tok_lane, prod.reshape(group, top_k, tok), 0.0), axis=0)
     gg_out[...] = gg
 
-    pairs[OWN].wait_recv()
-    own_out[...] = own_out[...] + pair_recv[OWN]
-    pairs[LEFT].wait_recv()
-    left_out[...] = left_out[...] + pair_recv[LEFT]
-    pairs[RIGHT].wait_recv()
-    right_out[...] = right_out[...] + pair_recv[RIGHT]
+    gy_wait(opp, quarter[0], 8)
+    gy_wait(opp, quarter[1], 9)
+    gy_send(opp, top, 17, sib)
+    gy_wait(opp, quarter[2], 10)
+    gy_wait(opp, quarter[3], 11)
+    gy_send(opp, bottom, 18, sib)
+    route_wait(5, 6)
+    build_rows(homes[OPP])
+    gy_wait(others[OPP], top, 17)
+    gy_wait(others[OPP], bottom, 18)
+    build_rows(others[OPP])
+    hidden_grads([OPP], 0, n_loc)
+
+    gy_wait(left, quarter[2], 2)
+    gy_wait(left, quarter[3], 3)
+    gy_send(left, bottom, 14, sib)
+    gy_wait(right, quarter[0], 6)
+    gy_wait(right, quarter[1], 7)
+    gy_send(right, top, 16, sib)
+
+    hops = []
+
+    def hop(i):
+        pairs["hop", i].wait_recv()
+        opp_keep[i] = opp_keep[i] + opp_recv[i]
+        for k, (part, dev) in enumerate(((top, right), (bottom, left))):
+            copy = remote(opp_keep.at[i, part], hop_recv.at[k, i], hop_ssem.at[k, i], hop_rsem.at[k, i], dev)
+            copy.start()
+            sends.append(copy)
+            hops.append((k, i, copy))
+
+    for i, n in enumerate(all_cols):
+        returned([OPP], 0, n_loc, [n])
+        opp_send[i] = token_sum(OPP, 1 - core, n)
+        send_pair(("hop", i), 6 + i, opp_send.at[i], opp_recv.at[i])
+        opp_keep[i] = token_sum(OPP, core, n)
+        if i > 1:
+            hop(i - 2)
+
+    near = ((LEFT, left_out), (RIGHT, right_out))
+    route_wait(1, 2, 3, 4)
+    build_rows(homes[LEFT])
+    hop(model // COLS - 2)
+    build_rows(homes[RIGHT])
+    hop(model // COLS - 1)
+    gy_wait(others[LEFT], top, 13)
+    gy_wait(others[LEFT], bottom, 14)
+    build_rows(others[LEFT])
+    gy_wait(others[RIGHT], bottom, 15)
+    gy_wait(others[RIGHT], top, 16)
+    build_rows(others[RIGHT])
+    hidden_grads([LEFT, RIGHT], 0, n_loc)
+    col_parts = (all_cols[:-1], all_cols[-1:])
+    add_pair(OWN, 0, all_cols, own_out)
+    for part, cols in enumerate(col_parts):
+        returned([LEFT, RIGHT], 0, n_loc, cols)
+        finish(cols, part, *near)
+    for part, cols in enumerate(col_parts):
+        for role, out in near:
+            add_pair(role, part, cols, out)
     for k, i, copy in hops:
         copy.wait_recv()
         out, part = ((right_out, top), (left_out, bottom))[k]
@@ -317,7 +350,6 @@
 def exchange(axis, n_dev, topk_idx, slot_ids, gate_vals, pair_counts, grad_y, y_rows, h_gate, h_up, w_gate, w_up, w_down):
     n_loc, n_rows, ffn = h_gate.shape
     tok, model = grad_y.shape
-    top_k = topk_idx.shape[0]
     cap = n_rows // n_dev
     vmem = pl.BlockSpec(memory_space=pltpu.VMEM)
     hbm = pl.BlockSpec(memory_space=pl.ANY)
@@ -330,7 +362,7 @@
             pltpu.VMEM((n_loc, n_rows, model), BF16),
             pltpu.VMEM((n_loc, n_rows, 2 * ffn), BF16),
             pltpu.VMEM((n_loc, n_rows, ffn), BF16),
-            pltpu.VMEM((top_k, tok), F32),
+            pltpu.VMEM((topk_idx.shape[0], tok), F32),
             part, part, part,
         ),
         in_specs=[vmem] * 4 + [hbm] * 7,
@@ -344,18 +376,20 @@
             pltpu.VMEM(h_up.shape, BF16),
             pltpu.VMEM((n_loc, model, 2 * ffn), BF16),
             pltpu.VMEM(w_down.shape, BF16),
+            pltpu.VMEM((n_loc, 2 * ffn, model), BF16),
+            pltpu.VMEM((n_loc, model, ffn), BF16),
             pltpu.VMEM(h_gate.shape, F32),
             pltpu.VMEM(h_gate.shape, F32),
             pltpu.VMEM((n_dev, n_loc * cap, tok), BF16),
-            pltpu.VMEM((n_dev, n_loc * cap, model), BF16),
-            pltpu.VMEM((4, tok, model), F32),
-            pltpu.VMEM((4, tok, model), F32),
+            pltpu.VMEM((4, n_loc * cap, model), BF16),
+            pltpu.VMEM((3, tok, model), F32),
+            pltpu.VMEM((3, tok, model), F32),
             pltpu.VMEM((model // COLS, tok, COLS), F32),
             pltpu.VMEM((model // COLS, tok, COLS), F32),
             pltpu.VMEM((model // COLS, tok, COLS), F32),
             pltpu.VMEM((2, model // COLS, tok // 2, COLS), F32),
-            dma((5 + 2 * n_loc,)), dma((n_dev - 1,)), dma((n_dev - 1,)), dma((13,)), dma((13,)),
-            dma((4 + model // COLS,)), dma((4 + model // COLS,)), dma((2, model // COLS)), dma((2, model // COLS)),
+            dma((5 + 2 * n_loc,)), dma((n_dev - 1,)), dma((n_dev - 1,)), dma((19,)), dma((19,)),
+            dma((6 + model // COLS,)), dma((6 + model // COLS,)), dma((2, model // COLS)), dma((2, model // COLS)),
         ],
         compiler_params=pltpu.CompilerParams(collective_id=0, has_side_effects=True, vmem_limit_bytes=EXCHANGE_VMEM),
     )(topk_idx, slot_ids, gate_vals, pair_counts, grad_y, y_rows, h_gate, h_up, w_gate, w_up, w_down)

time: 46.5 us -> 45.7 us (0.983)
  Pallas kernels: 42.3 us -> 41 us
  waiting for transfers between devices: 0.58 us -> 1.2 us
    pallas_call x1, Pallas kernels: 30.8 us -> 29.5 us  [exchange(): pl.pallas_call(functools.partial(exchange_kernel, axis, n_dev), name='exc...]
    ppermute x1, waiting for transfers between devices: 0.57 us -> 1.2 us  [local_step(): from_left = lax.ppermute(for_right, axis, to_right)]
  transfers between devices with their start and end apart: 2 -> 2, of which waited for: 1 -> 1; matrix products, arithmetic and copies ran while one was open for 0% -> 0% of each run, Pallas kernels for 23% -> 24%
where the time goes in v6:
time: 45.7 us; the launch traced here: 45.6 us
  Pallas kernels  41 us (90%)
  starting transfers between devices  2.76 us (6%)
  waiting for transfers between devices  1.2 us (3%)
  between operations  0.65 us (1%)
    pallas_call x1, Pallas kernels, exchange(): pl.pallas_call(functools.partial(exchange_kernel, axis, n_dev), name='exc...  29.5 us
    pallas_call x1, Pallas kernels, weight_grads(): pl.pallas_call(weight_kernel, name='weight_grads', in_specs=[hbm] + [vmem...  10.7 us
    ppermute x1, starting transfers between devices, local_step(): from_right = lax.ppermute(for_left, axis, to_left)  2.15 us
    ppermute x1, waiting for transfers between devices, local_step(): from_left = lax.ppermute(for_right, axis, to_right)  1.2 us
  transfers between devices with their start and end apart: 2, of which 1 were waited for; matrix products, arithmetic and copies ran while one was open for 0% of the time, Pallas kernels for 24%

profile of v6, /device:TPU:81, one launch (start us, length us, event | category | flops | bytes accessed | tf_op | source)
XLA Modules:
  0.0 45.6 jit_solution(6696558855420319519)
XLA Ops:
  0.6 29.5 %exchange.1 = (bf16[4,512,1024]{2,1,0:T(8,128)(2,1)S(1)}, bf16[4,512,1024]{2,1,0:T(8,128)(2,1)S(1)}, bf16[4,512,512]{2,1,0:T(8,128)(2,1)S(1)}, f32[8,128]{1,0:T(...) custom-call(s32[8,128]{1,0:T(8,128)} %bitcast.6, s32[8,128]{1,0:T(8,128)} %bitcast.7, ...), custom_call_target="tpu_custom_call" | custom-call | tf_op jit(solution)/shard_map/exchange/pallas_call | solution.py:358
  30.2 0.6 %collective-permute-start = (f32[128,1024]{1,0:T(8,128)S(1)}, f32[128,1024]{1,0:T(8,128)S(1)}, u32[]{:S(2)}, u32[]{:S(2)}) collective-permute-start(f32[128,1024]{1,0:T(8,128)S(1)} %get-tuple-element.17), channel_id=1, source_target_pairs={{0,2},{1,3},{2,4},{3,5},{4,6},{5,7},{6,0},{7,1},{8,10},{9,11},{10,... | collective-permute-start | bytes 1572872 | tf_op jit(solution)/shard_map/ppermute | solution.py:490
  30.8 2.1 %collective-permute-start.1 = (f32[128,1024]{1,0:T(8,128)S(1)}, f32[128,1024]{1,0:T(8,128)S(1)}, u32[]{:S(2)}, u32[]{:S(2)}) collective-permute-start(f32[128,1024]{1,0:T(8,128)S(1)} %get-tuple-element.18), channel_id=1, source_target_pairs={{0,6},{1,7},{2,0},{3,1},{4,2},{5,3},{6,4},{7,5},{8,14},{9,15},{10,... | collective-permute-start | bytes 1572872 | tf_op jit(solution)/shard_map/ppermute | solution.py:491
  32.9 10.7 %weight_grads.1 = (f32[4,1024,512]{2,1,0:T(8,128)}, f32[4,1024,512]{2,1,0:T(8,128)}, f32[4,512,1024]{2,1,0:T(8,128)}, f32[8,128]{1,0:T(8,128)}) custom-call(bf16[4,512,1024]{2,1,0:T(8,128)(2,1)} %x_hbm.1, bf16[4,512,1024]{2,1,0:T(8,128)(2,1)S(1)} %get-tuple-element.19.dh_buf, bf16[4,512,512]{2,1,0:T(8,128)(2,1)S(1)} %get-tuple-element.20.a_buf, ...), custom_call_target="tpu_custom_call" | custom-call | flops 6442450944 | bytes 29360128 | tf_op jit(solution)/shard_map/weight_grads/pallas_call | solution.py:437
  43.7 1.2 %collective-permute-done.left_ref = f32[128,1024]{1,0:T(8,128)S(1)} collective-permute-done((f32[128,1024]{1,0:T(8,128)S(1)}, f32[128,1024]{1,0:T(8,128)S(1)}, u32[]{:S(2)}, u32[]{:S(2)}) %collective-permute-start) | collective-permute-done | bytes 524320 | tf_op jit(solution)/shard_map/ppermute | solution.py:490
  44.9 0.0 collective-permute-done.1.right_ref
  44.9 0.8 %final_sum.1 = bf16[128,1024]{1,0:T(8,128)(2,1)} custom-call(f32[128,1024]{1,0:T(8,128)S(1)} %get-tuple-element.16.own_ref, f32[128,1024]{1,0:T(8,128)S(1)} %collective-permute-done.left_ref, f32[128,1024]{1,0:T(8,128)S(1)} %collective-permute-done.1.right_ref), custom_call_target="tpu_custom_call" | custom-call | tf_op jit(solution)/shard_map/final_sum/pallas_call | solution.py:467
Async XLA Ops:
  30.2 14.7 %collective-permute-start = (f32[128,1024]{1,0:T(8,128)S(1)}, f32[128,1024]{1,0:T(8,128)S(1)}, u32[]{:S(2)}, u32[]{:S(2)}) collective-permute-start(f32[128,1024]{1,0:T(8,128)S(1)} %get-tuple-element.17), channel_id=1, source_target_pairs={{0,2},{1,3},{2,4},{3,5},{4,6},{5,7},{6,0},{7,1},{8,10},{9,11},{10,... | collective-permute-start | bytes 1572872 | tf_op jit(solution)/shard_map/ppermute | solution.py:490
  30.8 14.1 %collective-permute-start.1 = (f32[128,1024]{1,0:T(8,128)S(1)}, f32[128,1024]{1,0:T(8,128)S(1)}, u32[]{:S(2)}, u32[]{:S(2)}) collective-permute-start(f32[128,1024]{1,0:T(8,128)S(1)} %get-tuple-element.18), channel_id=1, source_target_pairs={{0,6},{1,7},{2,0},{3,1},{4,2},{5,3},{6,4},{7,5},{8,14},{9,15},{10,... | collective-permute-start | bytes 1572872 | tf_op jit(solution)/shard_map/ppermute | solution.py:491

commit v7 on v6

--- a/solution.py
+++ b/solution.py
@@ -72,25 +72,19 @@
     def remote(src, dst, ssem, rsem, dev):
         return pltpu.make_async_remote_copy(src_ref=src, dst_ref=dst, send_sem=ssem, recv_sem=rsem, device_id={axis: dev}, device_id_type=pl.DeviceIdType.MESH)
 
-    sends = []
-
-    def gy_copy(block, part, send_slot, recv_slot, dev):
+    def gy_copy(block, part, recv_slot, dev):
         ref = gy_all.at[block, part]
-        return remote(ref, ref, gy_ssem.at[send_slot], gy_rsem.at[recv_slot], dev)
+        return remote(ref, ref, gy_ssem, gy_rsem.at[recv_slot], dev)
 
     def gy_send(block, part, recv_slot, dev):
-        copy = gy_copy(block, part, recv_slot, recv_slot, dev)
-        copy.start()
-        sends.append(copy)
+        gy_copy(block, part, recv_slot, dev).start()
 
     def gy_wait(block, part, recv_slot):
-        gy_copy(block, part, recv_slot, recv_slot, sib).wait_recv()
+        gy_copy(block, part, recv_slot, sib).wait_recv()
 
     gy_send(me, quarter[0], 0, right)
-    gy_send(me, quarter[2], 4, left)
-    gy_send(me, quarter[1], 1, right)
-    gy_send(me, quarter[3], 5, left)
-    gy_send(me, whole, 12, sib)
+    gy_send(me, quarter[2], 3, left)
+    gy_send(me, whole, 8, sib)
 
     topk_t = topk_ref[...].astype(F32)
     slot_t = slot_ref[...].astype(F32)
@@ -112,13 +106,11 @@
     route_all[me] = route_send[me]
 
     peers = [sib, left, others[LEFT], right, others[RIGHT], opp, others[OPP]]
-    arrives = [0, 3, 4, 1, 2, 5, 6]
     for k, dst in enumerate(peers):
-        copy = remote(route_send.at[dst], route_all.at[me], route_ssem.at[k], route_rsem.at[arrives[k]], dst)
-        copy.start()
-        sends.append(copy)
-    gy_send(me, quarter[2], 2, right)
-    gy_send(me, quarter[0], 6, left)
+        remote(route_send.at[dst], route_all.at[me], route_ssem, route_rsem.at[(k + 3) // 4], dst).start()
+    for to_right, to_left, slot in ((1, 3, 1), (2, 0, 2), (3, 1, 2)):
+        gy_send(me, quarter[to_right], slot, right)
+        gy_send(me, quarter[to_left], 3 + slot, left)
 
     chunk = 32
     n_chunk = n_rows // chunk
@@ -142,21 +134,22 @@
     for e in range(n_loc):
         factors(e)
 
-    def route_wait(*slots):
-        for k in slots:
-            remote(route_send.at[peers[k]], route_all.at[peers[k]], route_ssem.at[k], route_rsem.at[k], peers[k]).wait_recv()
+    def route_wait(slot, n):
+        blocks = route_all.at[pl.ds(0, n)]
+        remote(blocks, blocks, route_ssem, route_rsem.at[slot], sib).wait_recv()
 
     slot_iota = lax.broadcasted_iota(jnp.int32, (cap, tok), 0).astype(F32)
 
     def build_rows(s):
         route = route_all[s]
-        gates = []
+        picks, gates = [], []
         for e in range(n_loc):
             hit = route[e : e + 1] == slot_iota
-            oh_buf[s, pl.ds(e * cap, cap)] = jnp.where(hit, 1.0, 0.0).astype(BF16)
+            picks.append(jnp.where(hit, 1.0, 0.0).astype(BF16))
             gates.append(jnp.sum(jnp.where(hit, route[n_loc + e : n_loc + e + 1], 0.0), axis=1, keepdims=True))
         gate = jnp.concatenate(gates, axis=0)
-        pick = oh_buf[s]
+        pick = jnp.concatenate(picks, axis=0)
+        oh_buf[s] = pick.T
         for n in range(0, model, COLS):
             rows = (jnp.dot(pick, gy_all[s, :, pl.ds(n, COLS)], preferred_element_type=F32) * gate).astype(BF16)
             for e in range(n_loc):
@@ -216,55 +209,55 @@
     all_cols = range(0, model, COLS)
 
     def token_sum(role, k, n):
-        return dot_first(oh_buf[2 * chips[role] + k], r_buf[2 * (role == RIGHT) + k, :, pl.ds(n, COLS)])
-
-    pairs = {}
-
-    def send_pair(key, slot, ref_send, ref_recv):
-        pairs[key] = remote(ref_send, ref_recv, pair_ssem.at[slot], pair_rsem.at[slot], sib)
-        pairs[key].start()
-        sends.append(pairs[key])
-
-    def finish(cols, part, *roles):
+        return jnp.dot(oh_buf[2 * chips[role] + k], r_buf[2 * (role == RIGHT) + k, :, pl.ds(n, COLS)], preferred_element_type=F32)
+
+    def finish(cols, slot, *roles):
+        block = pl.ds(cols[0], len(cols) * COLS)
         for role, _ in roles:
             for n in cols:
                 pair_send[role - 1, :, pl.ds(n, COLS)] = token_sum(role, 1 - core, n)
-            block = pl.ds(cols[0], len(cols) * COLS)
-            send_pair((role, part), 2 * (role - 1) + part, pair_send.at[role - 1, :, block], pair_recv.at[role - 1, :, block])
+            remote(pair_send.at[role - 1, :, block], pair_recv.at[role - 1, :, block], pair_ssem.at[0], pair_rsem.at[slot], sib).start()
         for role, out in roles:
             for n in cols:
                 out[:, pl.ds(n, COLS)] = token_sum(role, core, n)
 
-    def add_pair(role, part, cols, out):
-        pairs[role, part].wait_recv()
+    def add_pair(cols, slot, *roles):
         block = pl.ds(cols[0], len(cols) * COLS)
-        out[:, block] = out[:, block] + pair_recv[role - 1, :, block]
+        first = roles[0][0] - 1
+        ref = pair_recv.at[pl.ds(first, len(roles)), :, block]
+        remote(ref, ref, pair_ssem.at[0], pair_rsem.at[slot], sib).wait_recv()
+        for role, out in roles:
+            out[:, block] = out[:, block] + pair_recv[role - 1, :, block]
 
     loads["wd"].wait()
-    route_wait(0)
-    gy_wait(others[OWN], whole, 12)
+    route_wait(0, 1)
+    gy_wait(others[OWN], whole, 8)
     build_rows(homes[OWN])
     build_rows(others[OWN])
-    hidden_grads([OWN], 0, n_loc - 1)
+    hidden_grads([OWN], 0, n_loc)
     gy_wait(left, quarter[0], 0)
-    gy_send(left, quarter[0], 8, right)
-    gy_wait(right, quarter[2], 4)
-    gy_send(right, quarter[2], 10, left)
-
-    hidden_grads([OWN], n_loc - 1, n_loc)
+    gy_send(left, quarter[0], 6, right)
+    gy_wait(right, quarter[2], 3)
+    gy_send(right, quarter[2], 7, left)
+
     loads["wg"].wait()
     loads["wu"].wait()
     returned([OWN], 0, 1, all_cols)
 
     gy_wait(left, quarter[1], 1)
-    gy_send(left, quarter[1], 9, right)
-    gy_send(me, quarter[3], 3, right)
-    gy_wait(right, quarter[3], 5)
-    gy_send(right, quarter[3], 11, left)
-    gy_send(me, quarter[1], 7, left)
-    gy_send(left, top, 13, sib)
-    gy_send(right, bottom, 15, sib)
+    gy_send(left, quarter[1], 6, right)
+    gy_send(left, top, 9, sib)
+    gy_wait(right, quarter[3], 4)
+    gy_send(right, quarter[3], 7, left)
+    gy_send(right, bottom, 10, sib)
+
     returned([OWN], 1, n_loc, all_cols)
+
+    gy_wait(left, bottom, 2)
+    gy_send(left, bottom, 9, sib)
+    gy_wait(right, top, 5)
+    gy_send(right, top, 10, sib)
+
     finish(all_cols, 0, (OWN, own_out))
 
     loads["y"].wait()
@@ -277,74 +270,63 @@
         gg += jnp.sum(jnp.where(tok_major + i * group == tok_lane, prod.reshape(group, top_k, tok), 0.0), axis=0)
     gg_out[...] = gg
 
-    gy_wait(opp, quarter[0], 8)
-    gy_wait(opp, quarter[1], 9)
-    gy_send(opp, top, 17, sib)
-    gy_wait(opp, quarter[2], 10)
-    gy_wait(opp, quarter[3], 11)
-    gy_send(opp, bottom, 18, sib)
-    route_wait(5, 6)
+    route_wait(1, 4)
+    build_rows(homes[LEFT])
+    build_rows(homes[RIGHT])
+    gy_wait(others[LEFT], whole, 9)
+    build_rows(others[LEFT])
+    gy_wait(others[RIGHT], whole, 10)
+    build_rows(others[RIGHT])
+
+    gy_wait(opp, top, 6)
+    gy_send(opp, top, 11, sib)
+    gy_wait(opp, bottom, 7)
+    gy_send(opp, bottom, 11, sib)
+    route_wait(2, 2)
     build_rows(homes[OPP])
-    gy_wait(others[OPP], top, 17)
-    gy_wait(others[OPP], bottom, 18)
+    hidden_grads([LEFT, RIGHT], 0, n_loc)
+
+    gy_wait(others[OPP], whole, 11)
     build_rows(others[OPP])
     hidden_grads([OPP], 0, n_loc)
 
-    gy_wait(left, quarter[2], 2)
-    gy_wait(left, quarter[3], 3)
-    gy_send(left, bottom, 14, sib)
-    gy_wait(right, quarter[0], 6)
-    gy_wait(right, quarter[1], 7)
-    gy_send(right, top, 16, sib)
-
-    hops = []
+    def opp_pair(i):
+        return remote(opp_send.at[i], opp_recv.at[i], pair_ssem.at[1], pair_rsem.at[3 + i], sib)
 
     def hop(i):
-        pairs["hop", i].wait_recv()
+        opp_pair(i).wait_recv()
         opp_keep[i] = opp_keep[i] + opp_recv[i]
         for k, (part, dev) in enumerate(((top, right), (bottom, left))):
-            copy = remote(opp_keep.at[i, part], hop_recv.at[k, i], hop_ssem.at[k, i], hop_rsem.at[k, i], dev)
-            copy.start()
-            sends.append(copy)
-            hops.append((k, i, copy))
+            remote(opp_keep.at[i, part], hop_recv.at[i, k], hop_ssem, hop_rsem.at[i], dev).start()
 
     for i, n in enumerate(all_cols):
         returned([OPP], 0, n_loc, [n])
         opp_send[i] = token_sum(OPP, 1 - core, n)
-        send_pair(("hop", i), 6 + i, opp_send.at[i], opp_recv.at[i])
+        opp_pair(i).start()
         opp_keep[i] = token_sum(OPP, core, n)
-        if i > 1:
-            hop(i - 2)
+        if i:
+            hop(i - 1)
 
     near = ((LEFT, left_out), (RIGHT, right_out))
-    route_wait(1, 2, 3, 4)
-    build_rows(homes[LEFT])
-    hop(model // COLS - 2)
-    build_rows(homes[RIGHT])
-    hop(model // COLS - 1)
-    gy_wait(others[LEFT], top, 13)
-    gy_wait(others[LEFT], bottom, 14)
-    build_rows(others[LEFT])
-    gy_wait(others[RIGHT], bottom, 15)
-    gy_wait(others[RIGHT], top, 16)
-    build_rows(others[RIGHT])
-    hidden_grads([LEFT, RIGHT], 0, n_loc)
     col_parts = (all_cols[:-1], all_cols[-1:])
-    add_pair(OWN, 0, all_cols, own_out)
+    add_pair(all_cols, 0, (OWN, own_out))
     for part, cols in enumerate(col_parts):
         returned([LEFT, RIGHT], 0, n_loc, cols)
-        finish(cols, part, *near)
+        if part == 0:
+            hop(model // COLS - 1)
+        finish(cols, 1 + part, *near)
     for part, cols in enumerate(col_parts):
-        for role, out in near:
-            add_pair(role, part, cols, out)
-    for k, i, copy in hops:
-        copy.wait_recv()
-        out, part = ((right_out, top), (left_out, bottom))[k]
-        cols = pl.ds(i * COLS, COLS)
-        out[part, cols] = out[part, cols] + hop_recv[k, i]
-
-    for copy in sends:
-        copy.wait_send()
+        add_pair(cols, 1 + part, *near)
+    for i, n in enumerate(all_cols):
+        remote(hop_recv.at[i], hop_recv.at[i], hop_ssem, hop_rsem.at[i], right).wait_recv()
+        cols = pl.ds(n, COLS)
+        right_out[top, cols] = right_out[top, cols] + hop_recv[i, 0]
+        left_out[bottom, cols] = left_out[bottom, cols] + hop_recv[i, 1]
+
+    sent = gy_all.at[pl.ds(0, n_dev - 1)]
+    for ref, ssem, rsem in ((sent, gy_ssem, gy_rsem), (route_all.at[pl.ds(0, n_dev - 1)], route_ssem, route_rsem), (pair_send, pair_ssem.at[0], pair_rsem),
+                            (opp_send, pair_ssem.at[1], pair_rsem), (hop_recv, hop_ssem, hop_rsem)):
+        remote(ref, ref, ssem, rsem.at[0], sib).wait_send()
 
 
 def exchange(axis, n_dev, topk_idx, slot_ids, gate_vals, pair_counts, grad_y, y_rows, h_gate, h_up, w_gate, w_up, w_down):
@@ -380,16 +362,15 @@
             pltpu.VMEM((n_loc, model, ffn), BF16),
             pltpu.VMEM(h_gate.shape, F32),
             pltpu.VMEM(h_gate.shape, F32),
-            pltpu.VMEM((n_dev, n_loc * cap, tok), BF16),
+            pltpu.VMEM((n_dev, tok, n_loc * cap), BF16),
             pltpu.VMEM((4, n_loc * cap, model), BF16),
             pltpu.VMEM((3, tok, model), F32),
             pltpu.VMEM((3, tok, model), F32),
             pltpu.VMEM((model // COLS, tok, COLS), F32),
             pltpu.VMEM((model // COLS, tok, COLS), F32),
             pltpu.VMEM((model // COLS, tok, COLS), F32),
-            pltpu.VMEM((2, model // COLS, tok // 2, COLS), F32),
-            dma((5 + 2 * n_loc,)), dma((n_dev - 1,)), dma((n_dev - 1,)), dma((19,)), dma((19,)),
-            dma((6 + model // COLS,)), dma((6 + model // COLS,)), dma((2, model // COLS)), dma((2, model // COLS)),
+            pltpu.VMEM((model // COLS, 2, tok // 2, COLS), F32),
+            dma((5 + 2 * n_loc,)), dma, dma((3,)), dma, dma((12,)), dma((2,)), dma((3 + model // COLS,)), dma, dma((model // COLS,)),
         ],
         compiler_params=pltpu.CompilerParams(collective_id=0, has_side_effects=True, vmem_limit_bytes=EXCHANGE_VMEM),
     )(topk_idx, slot_ids, gate_vals, pair_counts, grad_y, y_rows, h_gate, h_up, w_gate, w_up, w_down)

time: 45.7 us -> 45 us (0.985)
  waiting for transfers between devices: 1.2 us -> 0.67 us
    ppermute x1, waiting for transfers between devices: 1.2 us -> 0.67 us  [local_step(): from_left = lax.ppermute(for_right, axis, to_right)]
    ppermute x1, starting transfers between devices: 0.62 us -> 0.11 us  [local_step(): from_left = lax.ppermute(for_right, axis, to_right)]
    ppermute x1, starting transfers between devices: 2.15 us -> 2.65 us  [local_step(): from_right = lax.ppermute(for_left, axis, to_left)]
where the time goes in v7:
time: 45 us; the launch traced here: 44.8 us
  Pallas kernels  40.7 us (90%)
  starting transfers between devices  2.76 us (6%)
  waiting for transfers between devices  0.67 us (1%)
  between operations  0.66 us (1%)
    pallas_call x1, Pallas kernels, exchange(): pl.pallas_call(functools.partial(exchange_kernel, axis, n_dev), name='exc...  29.2 us
    pallas_call x1, Pallas kernels, weight_grads(): pl.pallas_call(weight_kernel, name='weight_grads', in_specs=[hbm] + [vmem...  10.7 us
    ppermute x1, starting transfers between devices, local_step(): from_right = lax.ppermute(for_left, axis, to_left)  2.65 us
  transfers between devices with their start and end apart: 2, of which 1 were waited for; matrix products, arithmetic and copies ran while one was open for 0% of the time, Pallas kernels for 24%

profile of v7, /device:TPU:81, one launch (start us, length us, event | category | flops | bytes accessed | tf_op | source)
XLA Modules:
  0.0 44.8 jit_solution(7707944553862513603)
XLA Ops:
  0.6 29.2 %exchange.1 = (bf16[4,512,1024]{2,1,0:T(8,128)(2,1)S(1)}, bf16[4,512,1024]{2,1,0:T(8,128)(2,1)S(1)}, bf16[4,512,512]{2,1,0:T(8,128)(2,1)S(1)}, f32[8,128]{1,0:T(...) custom-call(s32[8,128]{1,0:T(8,128)} %bitcast.6, s32[8,128]{1,0:T(8,128)} %bitcast.7, ...), custom_call_target="tpu_custom_call" | custom-call | tf_op jit(solution)/shard_map/exchange/pallas_call | solution.py:340
  29.9 0.1 collective-permute-start
  30.0 2.6 %collective-permute-start.1 = (f32[128,1024]{1,0:T(8,128)S(1)}, f32[128,1024]{1,0:T(8,128)S(1)}, u32[]{:S(2)}, u32[]{:S(2)}) collective-permute-start(f32[128,1024]{1,0:T(8,128)S(1)} %get-tuple-element.18), channel_id=1, source_target_pairs={{0,6},{1,7},{2,0},{3,1},{4,2},{5,3},{6,4},{7,5},{8,14},{9,15},{10,... | collective-permute-start | bytes 1572872 | tf_op jit(solution)/shard_map/ppermute | solution.py:472
  32.7 10.7 %weight_grads.1 = (f32[4,1024,512]{2,1,0:T(8,128)}, f32[4,1024,512]{2,1,0:T(8,128)}, f32[4,512,1024]{2,1,0:T(8,128)}, f32[8,128]{1,0:T(8,128)}) custom-call(bf16[4,512,1024]{2,1,0:T(8,128)(2,1)} %x_hbm.1, bf16[4,512,1024]{2,1,0:T(8,128)(2,1)S(1)} %get-tuple-element.19.dh_buf, bf16[4,512,512]{2,1,0:T(8,128)(2,1)S(1)} %get-tuple-element.20.a_buf, ...), custom_call_target="tpu_custom_call" | custom-call | flops 6442450944 | bytes 29360128 | tf_op jit(solution)/shard_map/weight_grads/pallas_call | solution.py:418
  43.4 0.7 %collective-permute-done.left_ref = f32[128,1024]{1,0:T(8,128)S(1)} collective-permute-done((f32[128,1024]{1,0:T(8,128)S(1)}, f32[128,1024]{1,0:T(8,128)S(1)}, u32[]{:S(2)}, u32[]{:S(2)}) %collective-permute-start) | collective-permute-done | bytes 524320 | tf_op jit(solution)/shard_map/ppermute | solution.py:471
  44.1 0.0 collective-permute-done.1.right_ref
  44.1 0.8 %final_sum.1 = bf16[128,1024]{1,0:T(8,128)(2,1)} custom-call(f32[128,1024]{1,0:T(8,128)S(1)} %get-tuple-element.16.own_ref, f32[128,1024]{1,0:T(8,128)S(1)} %collective-permute-done.left_ref, f32[128,1024]{1,0:T(8,128)S(1)} %collective-permute-done.1.right_ref), custom_call_target="tpu_custom_call" | custom-call | tf_op jit(solution)/shard_map/final_sum/pallas_call | solution.py:448
Async XLA Ops:
  29.9 14.2 %collective-permute-start = (f32[128,1024]{1,0:T(8,128)S(1)}, f32[128,1024]{1,0:T(8,128)S(1)}, u32[]{:S(2)}, u32[]{:S(2)}) collective-permute-start(f32[128,1024]{1,0:T(8,128)S(1)} %get-tuple-element.17), channel_id=1, source_target_pairs={{0,2},{1,3},{2,4},{3,5},{4,6},{5,7},{6,0},{7,1},{8,10},{9,11},{10,... | collective-permute-start | bytes 1572872 | tf_op jit(solution)/shard_map/ppermute | solution.py:471
  30.0 14.0 %collective-permute-start.1 = (f32[128,1024]{1,0:T(8,128)S(1)}, f32[128,1024]{1,0:T(8,128)S(1)}, u32[]{:S(2)}, u32[]{:S(2)}) collective-permute-start(f32[128,1024]{1,0:T(8,128)S(1)} %get-tuple-element.18), channel_id=1, source_target_pairs={{0,6},{1,7},{2,0},{3,1},{4,2},{5,3},{6,4},{7,5},{8,14},{9,15},{10,... | collective-permute-start | bytes 1572872 | tf_op jit(solution)/shard_map/ppermute | solution.py:472

commit v8 on v7

--- a/solution.py
+++ b/solution.py
@@ -237,29 +237,73 @@
     hidden_grads([OWN], 0, n_loc)
     gy_wait(left, quarter[0], 0)
     gy_send(left, quarter[0], 6, right)
-    gy_wait(right, quarter[2], 3)
-    gy_send(right, quarter[2], 7, left)
 
     loads["wg"].wait()
     loads["wu"].wait()
     returned([OWN], 0, 1, all_cols)
-
+    gy_wait(right, quarter[2], 3)
+    gy_send(right, quarter[2], 7, left)
     gy_wait(left, quarter[1], 1)
     gy_send(left, quarter[1], 6, right)
     gy_send(left, top, 9, sib)
+
+    returned([OWN], 1, 2, all_cols)
     gy_wait(right, quarter[3], 4)
     gy_send(right, quarter[3], 7, left)
     gy_send(right, bottom, 10, sib)
 
-    returned([OWN], 1, n_loc, all_cols)
-
+    returned([OWN], 2, n_loc, all_cols)
     gy_wait(left, bottom, 2)
     gy_send(left, bottom, 9, sib)
+    finish(all_cols, 0, (OWN, own_out))
     gy_wait(right, top, 5)
     gy_send(right, top, 10, sib)
 
-    finish(all_cols, 0, (OWN, own_out))
-
+    route_wait(1, 4)
+    build_rows(homes[LEFT])
+    build_rows(homes[RIGHT])
+    gy_wait(others[LEFT], whole, 9)
+    build_rows(others[LEFT])
+    gy_wait(others[RIGHT], whole, 10)
+    build_rows(others[RIGHT])
+
+    gy_wait(opp, top, 6)
+    gy_send(opp, top, 11, sib)
+    gy_wait(opp, bottom, 7)
+    gy_send(opp, bottom, 11, sib)
+    route_wait(2, 2)
+    build_rows(homes[OPP])
+    hidden_grads([LEFT, RIGHT], 0, n_loc)
+
+    gy_wait(others[OPP], whole, 11)
+    build_rows(others[OPP])
+    hidden_grads([OPP], 0, n_loc)
+
+    def opp_pair(i):
+        return remote(opp_send.at[i], opp_recv.at[i], pair_ssem.at[1], pair_rsem.at[3 + i], sib)
+
+    def hop(i):
+        opp_pair(i).wait_recv()
+        opp_keep[i] = opp_keep[i] + opp_recv[i]
+        for k, (part, dev) in enumerate(((top, right), (bottom, left))):
+            remote(opp_keep.at[i, part], hop_recv.at[i, k], hop_ssem, hop_rsem.at[i], dev).start()
+
+    for i, n in enumerate(all_cols):
+        returned([OPP], 0, n_loc, [n])
+        opp_send[i] = token_sum(OPP, 1 - core, n)
+        opp_pair(i).start()
+        opp_keep[i] = token_sum(OPP, core, n)
+        if i:
+            hop(i - 1)
+
+    near = ((LEFT, left_out), (RIGHT, right_out))
+    col_parts = (all_cols[:-1], all_cols[-1:])
+    add_pair(all_cols, 0, (OWN, own_out))
+    for part, cols in enumerate(col_parts):
+        returned([LEFT, RIGHT], 0, n_loc, cols)
+        if part == 0:
+            hop(model // COLS - 1)
+        finish(cols, 1 + part, *near)
     loads["y"].wait()
     group = 32
     gg = jnp.zeros((top_k, tok), F32)
@@ -270,51 +314,6 @@
         gg += jnp.sum(jnp.where(tok_major + i * group == tok_lane, prod.reshape(group, top_k, tok), 0.0), axis=0)
     gg_out[...] = gg
 
-    route_wait(1, 4)
-    build_rows(homes[LEFT])
-    build_rows(homes[RIGHT])
-    gy_wait(others[LEFT], whole, 9)
-    build_rows(others[LEFT])
-    gy_wait(others[RIGHT], whole, 10)
-    build_rows(others[RIGHT])
-
-    gy_wait(opp, top, 6)
-    gy_send(opp, top, 11, sib)
-    gy_wait(opp, bottom, 7)
-    gy_send(opp, bottom, 11, sib)
-    route_wait(2, 2)
-    build_rows(homes[OPP])
-    hidden_grads([LEFT, RIGHT], 0, n_loc)
-
-    gy_wait(others[OPP], whole, 11)
-    build_rows(others[OPP])
-    hidden_grads([OPP], 0, n_loc)
-
-    def opp_pair(i):
-        return remote(opp_send.at[i], opp_recv.at[i], pair_ssem.at[1], pair_rsem.at[3 + i], sib)
-
-    def hop(i):
-        opp_pair(i).wait_recv()
-        opp_keep[i] = opp_keep[i] + opp_recv[i]
-        for k, (part, dev) in enumerate(((top, right), (bottom, left))):
-            remote(opp_keep.at[i, part], hop_recv.at[i, k], hop_ssem, hop_rsem.at[i], dev).start()
-
-    for i, n in enumerate(all_cols):
-        returned([OPP], 0, n_loc, [n])
-        opp_send[i] = token_sum(OPP, 1 - core, n)
-        opp_pair(i).start()
-        opp_keep[i] = token_sum(OPP, core, n)
-        if i:
-            hop(i - 1)
-
-    near = ((LEFT, left_out), (RIGHT, right_out))
-    col_parts = (all_cols[:-1], all_cols[-1:])
-    add_pair(all_cols, 0, (OWN, own_out))
-    for part, cols in enumerate(col_parts):
-        returned([LEFT, RIGHT], 0, n_loc, cols)
-        if part == 0:
-            hop(model // COLS - 1)
-        finish(cols, 1 + part, *near)
     for part, cols in enumerate(col_parts):
         add_pair(cols, 1 + part, *near)
     for i, n in enumerate(all_cols):

time: 45 us -> 45 us (level)
  no operation moved by 1% of the time
where the time goes in v8:
time: 45 us; the launch traced here: 44.8 us
  Pallas kernels  40.7 us (90%)
  starting transfers between devices  2.76 us (6%)
  waiting for transfers between devices  0.66 us (1%)
  between operations  0.66 us (1%)
    pallas_call x1, Pallas kernels, exchange(): pl.pallas_call(functools.partial(exchange_kernel, axis, n_dev), name='exc...  29.2 us
    pallas_call x1, Pallas kernels, weight_grads(): pl.pallas_call(weight_kernel, name='weight_grads', in_specs=[hbm] + [vmem...  10.7 us
    ppermute x1, starting transfers between devices, local_step(): from_right = lax.ppermute(for_left, axis, to_left)  2.65 us
  transfers between devices with their start and end apart: 2, of which 1 were waited for; matrix products, arithmetic and copies ran while one was open for 0% of the time, Pallas kernels for 24%

profile of v8, /device:TPU:81, one launch (start us, length us, event | category | flops | bytes accessed | tf_op | source)
XLA Modules:
  0.0 44.8 jit_solution(11149719357316447269)
XLA Ops:
  0.6 29.2 %exchange.1 = (bf16[4,512,1024]{2,1,0:T(8,128)(2,1)S(1)}, bf16[4,512,1024]{2,1,0:T(8,128)(2,1)S(1)}, bf16[4,512,512]{2,1,0:T(8,128)(2,1)S(1)}, f32[8,128]{1,0:T(...) custom-call(s32[8,128]{1,0:T(8,128)} %bitcast.6, s32[8,128]{1,0:T(8,128)} %bitcast.7, ...), custom_call_target="tpu_custom_call" | custom-call | tf_op jit(solution)/shard_map/exchange/pallas_call | solution.py:339
  29.9 0.1 collective-permute-start
  30.0 2.6 %collective-permute-start.1 = (f32[128,1024]{1,0:T(8,128)S(1)}, f32[128,1024]{1,0:T(8,128)S(1)}, u32[]{:S(2)}, u32[]{:S(2)}) collective-permute-start(f32[128,1024]{1,0:T(8,128)S(1)} %get-tuple-element.18), channel_id=1, source_target_pairs={{0,6},{1,7},{2,0},{3,1},{4,2},{5,3},{6,4},{7,5},{8,14},{9,15},{10,... | collective-permute-start | bytes 1572872 | tf_op jit(solution)/shard_map/ppermute | solution.py:471
  32.6 10.7 %weight_grads.1 = (f32[4,1024,512]{2,1,0:T(8,128)}, f32[4,1024,512]{2,1,0:T(8,128)}, f32[4,512,1024]{2,1,0:T(8,128)}, f32[8,128]{1,0:T(8,128)}) custom-call(bf16[4,512,1024]{2,1,0:T(8,128)(2,1)} %x_hbm.1, bf16[4,512,1024]{2,1,0:T(8,128)(2,1)S(1)} %get-tuple-element.19.dh_buf, bf16[4,512,512]{2,1,0:T(8,128)(2,1)S(1)} %get-tuple-element.20.a_buf, ...), custom_call_target="tpu_custom_call" | custom-call | flops 6442450944 | bytes 29360128 | tf_op jit(solution)/shard_map/weight_grads/pallas_call | solution.py:417
  43.4 0.7 %collective-permute-done.left_ref = f32[128,1024]{1,0:T(8,128)S(1)} collective-permute-done((f32[128,1024]{1,0:T(8,128)S(1)}, f32[128,1024]{1,0:T(8,128)S(1)}, u32[]{:S(2)}, u32[]{:S(2)}) %collective-permute-start) | collective-permute-done | bytes 524320 | tf_op jit(solution)/shard_map/ppermute | solution.py:470
  44.0 0.0 collective-permute-done.1.right_ref
  44.0 0.8 %final_sum.1 = bf16[128,1024]{1,0:T(8,128)(2,1)} custom-call(f32[128,1024]{1,0:T(8,128)S(1)} %get-tuple-element.16.own_ref, f32[128,1024]{1,0:T(8,128)S(1)} %collective-permute-done.left_ref, f32[128,1024]{1,0:T(8,128)S(1)} %collective-permute-done.1.right_ref), custom_call_target="tpu_custom_call" | custom-call | tf_op jit(solution)/shard_map/final_sum/pallas_call | solution.py:447
Async XLA Ops:
  29.9 14.2 %collective-permute-start = (f32[128,1024]{1,0:T(8,128)S(1)}, f32[128,1024]{1,0:T(8,128)S(1)}, u32[]{:S(2)}, u32[]{:S(2)}) collective-permute-start(f32[128,1024]{1,0:T(8,128)S(1)} %get-tuple-element.17), channel_id=1, source_target_pairs={{0,2},{1,3},{2,4},{3,5},{4,6},{5,7},{6,0},{7,1},{8,10},{9,11},{10,... | collective-permute-start | bytes 1572872 | tf_op jit(solution)/shard_map/ppermute | solution.py:470
  30.0 14.1 %collective-permute-start.1 = (f32[128,1024]{1,0:T(8,128)S(1)}, f32[128,1024]{1,0:T(8,128)S(1)}, u32[]{:S(2)}, u32[]{:S(2)}) collective-permute-start(f32[128,1024]{1,0:T(8,128)S(1)} %get-tuple-element.18), channel_id=1, source_target_pairs={{0,6},{1,7},{2,0},{3,1},{4,2},{5,3},{6,4},{7,5},{8,14},{9,15},{10,... | collective-permute-start | bytes 1572872 | tf_op jit(solution)/shard_map/ppermute | solution.py:471

commit v9 on v8

--- a/solution.py
+++ b/solution.py
@@ -273,7 +273,7 @@
     gy_send(opp, bottom, 11, sib)
     route_wait(2, 2)
     build_rows(homes[OPP])
-    hidden_grads([LEFT, RIGHT], 0, n_loc)
+    hidden_grads([LEFT, RIGHT], 0, n_loc // 2)
 
     gy_wait(others[OPP], whole, 11)
     build_rows(others[OPP])
@@ -299,10 +299,10 @@
     near = ((LEFT, left_out), (RIGHT, right_out))
     col_parts = (all_cols[:-1], all_cols[-1:])
     add_pair(all_cols, 0, (OWN, own_out))
+    hidden_grads([LEFT, RIGHT], n_loc // 2, n_loc)
+    hop(model // COLS - 1)
     for part, cols in enumerate(col_parts):
         returned([LEFT, RIGHT], 0, n_loc, cols)
-        if part == 0:
-            hop(model // COLS - 1)
         finish(cols, 1 + part, *near)
     loads["y"].wait()
     group = 32

time: 45 us -> 44.1 us (0.980)
  Pallas kernels: 40.7 us -> 39.9 us
    pallas_call x1, Pallas kernels: 29.2 us -> 28.4 us  [exchange(): pl.pallas_call(functools.partial(exchange_kernel, axis, n_dev), name='exc...]
  transfers between devices with their start and end apart: 2 -> 2, of which waited for: 1 -> 1; matrix products, arithmetic and copies ran while one was open for 0% -> 0% of each run, Pallas kernels for 24% -> 25%
where the time goes in v9:
time: 44.1 us; the launch traced here: 43.7 us
  Pallas kernels  39.9 us (90%)
  starting transfers between devices  2.76 us (6%)
  between operations  0.65 us (1%)
    pallas_call x1, Pallas kernels, exchange(): pl.pallas_call(functools.partial(exchange_kernel, axis, n_dev), name='exc...  28.4 us
    pallas_call x1, Pallas kernels, weight_grads(): pl.pallas_call(weight_kernel, name='weight_grads', in_specs=[hbm] + [vmem...  10.7 us
    ppermute x1, starting transfers between devices, local_step(): from_right = lax.ppermute(for_left, axis, to_left)  2.28 us
  transfers between devices with their start and end apart: 2, of which 1 were waited for; matrix products, arithmetic and copies ran while one was open for 0% of the time, Pallas kernels for 25%

profile of v9, /device:TPU:81, one launch (start us, length us, event | category | flops | bytes accessed | tf_op | source)
XLA Modules:
  0.0 43.7 jit_solution(11867197460312036284)
XLA Ops:
  0.6 28.4 %exchange.1 = (bf16[4,512,1024]{2,1,0:T(8,128)(2,1)S(1)}, bf16[4,512,1024]{2,1,0:T(8,128)(2,1)S(1)}, bf16[4,512,512]{2,1,0:T(8,128)(2,1)S(1)}, f32[8,128]{1,0:T(...) custom-call(s32[8,128]{1,0:T(8,128)} %bitcast.6, s32[8,128]{1,0:T(8,128)} %bitcast.7, ...), custom_call_target="tpu_custom_call" | custom-call | tf_op jit(solution)/shard_map/exchange/pallas_call | solution.py:339
  29.0 0.5 %collective-permute-start = (f32[128,1024]{1,0:T(8,128)S(1)}, f32[128,1024]{1,0:T(8,128)S(1)}, u32[]{:S(2)}, u32[]{:S(2)}) collective-permute-start(f32[128,1024]{1,0:T(8,128)S(1)} %get-tuple-element.17), channel_id=1, source_target_pairs={{0,2},{1,3},{2,4},{3,5},{4,6},{5,7},{6,0},{7,1},{8,10},{9,11},{10,... | collective-permute-start | bytes 1572872 | tf_op jit(solution)/shard_map/ppermute | solution.py:470
  29.5 2.3 %collective-permute-start.1 = (f32[128,1024]{1,0:T(8,128)S(1)}, f32[128,1024]{1,0:T(8,128)S(1)}, u32[]{:S(2)}, u32[]{:S(2)}) collective-permute-start(f32[128,1024]{1,0:T(8,128)S(1)} %get-tuple-element.18), channel_id=1, source_target_pairs={{0,6},{1,7},{2,0},{3,1},{4,2},{5,3},{6,4},{7,5},{8,14},{9,15},{10,... | collective-permute-start | bytes 1572872 | tf_op jit(solution)/shard_map/ppermute | solution.py:471
  31.8 10.7 %weight_grads.1 = (f32[4,1024,512]{2,1,0:T(8,128)}, f32[4,1024,512]{2,1,0:T(8,128)}, f32[4,512,1024]{2,1,0:T(8,128)}, f32[8,128]{1,0:T(8,128)}) custom-call(bf16[4,512,1024]{2,1,0:T(8,128)(2,1)} %x_hbm.1, bf16[4,512,1024]{2,1,0:T(8,128)(2,1)S(1)} %get-tuple-element.19.dh_buf, bf16[4,512,512]{2,1,0:T(8,128)(2,1)S(1)} %get-tuple-element.20.a_buf, ...), custom_call_target="tpu_custom_call" | custom-call | flops 6442450944 | bytes 29360128 | tf_op jit(solution)/shard_map/weight_grads/pallas_call | solution.py:417
  42.5 0.4 collective-permute-done.left_ref
  42.9 0.0 collective-permute-done.1.right_ref
  42.9 0.8 %final_sum.1 = bf16[128,1024]{1,0:T(8,128)(2,1)} custom-call(f32[128,1024]{1,0:T(8,128)S(1)} %get-tuple-element.16.own_ref, f32[128,1024]{1,0:T(8,128)S(1)} %collective-permute-done.left_ref, f32[128,1024]{1,0:T(8,128)S(1)} %collective-permute-done.1.right_ref), custom_call_target="tpu_custom_call" | custom-call | tf_op jit(solution)/shard_map/final_sum/pallas_call | solution.py:447
Async XLA Ops:
  29.0 13.9 %collective-permute-start = (f32[128,1024]{1,0:T(8,128)S(1)}, f32[128,1024]{1,0:T(8,128)S(1)}, u32[]{:S(2)}, u32[]{:S(2)}) collective-permute-start(f32[128,1024]{1,0:T(8,128)S(1)} %get-tuple-element.17), channel_id=1, source_target_pairs={{0,2},{1,3},{2,4},{3,5},{4,6},{5,7},{6,0},{7,1},{8,10},{9,11},{10,... | collective-permute-start | bytes 1572872 | tf_op jit(solution)/shard_map/ppermute | solution.py:470
  29.5 13.4 %collective-permute-start.1 = (f32[128,1024]{1,0:T(8,128)S(1)}, f32[128,1024]{1,0:T(8,128)S(1)}, u32[]{:S(2)}, u32[]{:S(2)}) collective-permute-start(f32[128,1024]{1,0:T(8,128)S(1)} %get-tuple-element.18), channel_id=1, source_target_pairs={{0,6},{1,7},{2,0},{3,1},{4,2},{5,3},{6,4},{7,5},{8,14},{9,15},{10,... | collective-permute-start | bytes 1572872 | tf_op jit(solution)/shard_map/ppermute | solution.py:471
